TPU v7x, 32 devices: a whole 2x2x4 slice. The times are simulated.
32 devices in a mesh: gy: 8 (over z, y), gz: 4 (over x, core).
Axes of the slice: x: 2, y: 2, z: 4, core: 2. Of those that a mesh axis runs over, the one named last changes fastest.
Arguments:
- eddy_cells: int32 [8, 4, 2, 2048], P('gy', 'gz'), may hold values from 0 to 16383, as said below
- eddy_signs: int32 [8, 4, 3, 2048], P('gy', 'gz'), may hold values from -1 to 1, as said below
- eddy_counts: int32 [8, 4], P('gy', 'gz'), may hold values from 256 to 2048
- stress_diag: float32 [3, 16384], P(None, 'gy'), may hold values from 0.3 to 3
- stress_shear: float32 [3, 16384], P(None, 'gy'), may hold values from -3 to 3
- mean_flow: float32 [3, 16384, 1024], P(None, 'gy', 'gz'), may hold values from -6 to 6
Outputs:
- velocity: float32 [3, 16384, 1024], P(None, 'gy', 'gz')
Inputs may be any that keep to these rules, and one draw needn't show every extreme that they name: `eddy_cells`: every slot of tile (i, j) holds a wall-normal cell in [i * 2048, (i + 1) * 2048) and a spanwise cell in [j * 256, (j + 1) * 256); only the first eddy_counts[i, j] slots are eddies. `eddy_signs`: each entry is -1 or 1.
All inputs are finite; a program needn't handle non-finite values.
Results may differ from a plain program's by a relative error of at most 0.0001.
Values sent between devices are 32-bit elements; how exact they have to be, the bound alone decides.
No kernel may reach another device: no remote copies, remote signals or barrier semaphores. Data moves between devices by JAX's collectives and lax.ppermute only.
A program may use at most 128 MiB of HBM per device.

v0:
```python
import math

import jax
import jax.numpy as jnp
from jax import lax
from jax.sharding import PartitionSpec as P

TY = 2048
TZ = 256
CAP = 2048
HALF = 128


shape_peak = math.sqrt(1.5)


def passed_along(value, axis, by):
    peers = lax.axis_size(axis)
    pairs = [(i, i + by) for i in range(peers) if 0 <= i + by < peers]
    return lax.ppermute(value, axis, pairs)


def passed_along_2(value, axis, by):
    peers = lax.axis_size(axis)
    return lax.ppermute(value, axis, [(i, (i + by) % peers) for i in range(peers)])


def profile(offsets):
    return shape_peak * jnp.maximum(1.0 - jnp.abs(offsets).astype(jnp.float32) / HALF, 0.0)


def tile_field(
    positions, signs_here, slot_low, slot_high, row_anchor, col_anchor, first_block, end_block
):
    block_size = min(256, CAP)
    ext_rows = TY + 2 * HALF
    ext_cols = TZ + 2 * HALF
    row_cells = row_anchor - HALF + jnp.arange(ext_rows, dtype=jnp.int32)
    col_cells = col_anchor - HALF + jnp.arange(ext_cols, dtype=jnp.int32)

    def add_block(block_index, running):
        first_slot = (block_index * block_size).astype(jnp.int32)
        slot_index = first_slot + jnp.arange(block_size, dtype=jnp.int32)
        places = lax.dynamic_slice_in_dim(positions, first_slot, block_size, 1)
        weights = lax.dynamic_slice_in_dim(signs_here, first_slot, block_size, 1).astype(
            jnp.float32
        )
        inside = jnp.logical_and(slot_index < slot_high, slot_index >= slot_low)
        weights = weights * inside.astype(jnp.float32)[None, :]
        wall_profile = profile(row_cells[:, None] - places[0][None, :])
        span_profile = profile(col_cells[:, None] - places[1][None, :])
        signed = (weights[:, None, :] * wall_profile[None, :, :]).reshape(3 * ext_rows, block_size)
        return running + lax.dot_general(
            signed,
            span_profile,
            (((1,), (1,)), ((), ())),
            precision=lax.Precision.HIGHEST,
            preferred_element_type=jnp.float32,
        )

    initial = jnp.zeros((3 * ext_rows, ext_cols), jnp.float32)
    return lax.fori_loop(first_block, end_block, add_block, initial).reshape(3, ext_rows, ext_cols)


def rescale(raw_field, stress_diag, stress_shear, mean_flow, amplitude):
    streamwise = stress_diag[0][:, None] * raw_field[0]
    normal_part = stress_shear[0][:, None] * raw_field[0] + stress_diag[1][:, None] * raw_field[1]
    spanwise = (
        stress_shear[1][:, None] * raw_field[0]
        + stress_shear[2][:, None] * raw_field[1]
        + stress_diag[2][:, None] * raw_field[2]
    )
    return mean_flow + amplitude * jnp.stack([streamwise, normal_part, spanwise])


def body(eddy_cells, eddy_signs, eddy_counts, stress_diag, stress_shear, mean_flow):
    live_count = eddy_counts.reshape(())
    eddy_total = lax.psum(live_count.astype(jnp.float32), ("gy", "gz"))
    positions = eddy_cells.reshape(2, CAP)
    signs_here = eddy_signs.reshape(3, CAP)
    block_size = min(256, CAP)
    row_anchor = lax.axis_index("gy") * TY
    col_anchor = lax.axis_index("gz") * TZ
    zero_block = jnp.int32(0)
    block_count = (live_count + block_size - 1) // block_size
    extended = tile_field(
        positions,
        signs_here,
        zero_block,
        live_count,
        row_anchor,
        col_anchor,
        zero_block,
        block_count,
    )
    from_below = passed_along(extended[:, :HALF, HALF : HALF + TZ], "gy", -1)
    from_above = passed_along(extended[:, TY + HALF :, HALF : HALF + TZ], "gy", 1)
    from_right = passed_along_2(extended[:, HALF : HALF + TY, :HALF], "gz", -1)
    from_left = passed_along_2(extended[:, HALF : HALF + TY, TZ + HALF :], "gz", 1)
    below_corners = passed_along(
        (extended[:, :HALF, :HALF], extended[:, :HALF, TZ + HALF :]), "gy", -1
    )
    above_corners = passed_along(
        (extended[:, TY + HALF :, :HALF], extended[:, TY + HALF :, TZ + HALF :]), "gy", 1
    )
    leftward = passed_along_2((below_corners[0], above_corners[0]), "gz", -1)
    rightward = passed_along_2((below_corners[1], above_corners[1]), "gz", 1)
    interior = extended[:, HALF : HALF + TY, HALF : HALF + TZ]
    interior = interior.at[:, TY - HALF :, :].add(from_below)
    interior = interior.at[:, :HALF, :].add(from_above)
    interior = interior.at[:, :, TZ - HALF :].add(from_right)
    interior = interior.at[:, :, :HALF].add(from_left)
    interior = interior.at[:, TY - HALF :, TZ - HALF :].add(leftward[0])
    interior = interior.at[:, :HALF, TZ - HALF :].add(leftward[1])
    interior = interior.at[:, TY - HALF :, :HALF].add(rightward[0])
    interior = interior.at[:, :HALF, :HALF].add(rightward[1])
    amplitude = jnp.sqrt(
        TY * lax.axis_size("gy") * (TZ * lax.axis_size("gz")) / (HALF * HALF) / eddy_total
    )
    return rescale(interior, stress_diag, stress_shear, mean_flow, amplitude)


def solution(mesh):
    in_specs = (
        P("gy", "gz", None, None),
        P("gy", "gz", None, None),
        P("gy", "gz"),
        P(None, "gy"),
        P(None, "gy"),
        P(None, "gy", "gz"),
    )
    out_specs = P(None, "gy", "gz")
    return jax.shard_map(body, mesh=mesh, in_specs=in_specs, out_specs=out_specs, check_vma=False)
```

profile of v0, /device:TPU:0, one launch (start us, length us, event | category | flops | bytes accessed | tf_op | source)
XLA Modules:
  0.0 330.6 jit_solution(13624741348397634622)
XLA Ops:
  1.4 6.8 %broadcast_in_dim.2 = f32[6912,512]{1,0:T(8,128)} broadcast(f32[]{:T(128)} %constant.271.clone.1), dimensions={} | broadcast | bytes 14155780 | tf_op jit(solution)/shard_map/broadcast_in_dim | solution.py:61
  8.3 118.1 %while.19 = (s32[]{:T(128)}, f32[6912,512]{1,0:T(8,128)}, s32[]{:T(128)}, s32[3,2048]{1,0:T(4,128)S(1)}, s32[]{:T(128)}, /*index=5*/s32[2,2048]{1,0:T(2,128)}, s...) while((s32[]{:T(128)}, f32[6912,512]{1,0:T(8,128)}, ...), condition=%wide.region_2.3_spmd.clone, body=%wide.region_1.2_spmd.clone.sunk | while | flops 10881996800 | bytes 47226064 | solution.py:62
  11.2 16.8 %convolution_add_fusion.2 = f32[6912,512]{1,0:T(8,128)} fusion(f32[6912,512]{1,0:T(8,128)} %get-tuple-element.272, f32[6912,256]{1,0:T(8,128)S(1)} %bitcast.28, s32[256]{0:T(256)S(1)} %bitcast.36, s32[512]{0:T(512)S(1)} %iota_add_fusion.5), kind=kOutput, calls=%fused_computation.2.clone.1 | convolution fusion | flops 10876092416 | bytes 35392512 | tf_op jit(solution)/shard_map/while/body/dot_general | solution.py:53
  30.9 16.8 %convolution_add_fusion.2 = f32[6912,512]{1,0:T(8,128)} fusion(f32[6912,512]{1,0:T(8,128)} %get-tuple-element.272, f32[6912,256]{1,0:T(8,128)S(1)} %bitcast.28, s32[256]{0:T(256)S(1)} %bitcast.36, s32[512]{0:T(512)S(1)} %iota_add_fusion.5), kind=kOutput, calls=%fused_computation.2.clone.1 | convolution fusion | flops 10876092416 | bytes 35392512 | tf_op jit(solution)/shard_map/while/body/dot_general | solution.py:53
  50.5 16.8 %convolution_add_fusion.2 = f32[6912,512]{1,0:T(8,128)} fusion(f32[6912,512]{1,0:T(8,128)} %get-tuple-element.272, f32[6912,256]{1,0:T(8,128)S(1)} %bitcast.28, s32[256]{0:T(256)S(1)} %bitcast.36, s32[512]{0:T(512)S(1)} %iota_add_fusion.5), kind=kOutput, calls=%fused_computation.2.clone.1 | convolution fusion | flops 10876092416 | bytes 35392512 | tf_op jit(solution)/shard_map/while/body/dot_general | solution.py:53
  70.2 16.8 %convolution_add_fusion.2 = f32[6912,512]{1,0:T(8,128)} fusion(f32[6912,512]{1,0:T(8,128)} %get-tuple-element.272, f32[6912,256]{1,0:T(8,128)S(1)} %bitcast.28, s32[256]{0:T(256)S(1)} %bitcast.36, s32[512]{0:T(512)S(1)} %iota_add_fusion.5), kind=kOutput, calls=%fused_computation.2.clone.1 | convolution fusion | flops 10876092416 | bytes 35392512 | tf_op jit(solution)/shard_map/while/body/dot_general | solution.py:53
  89.9 16.8 %convolution_add_fusion.2 = f32[6912,512]{1,0:T(8,128)} fusion(f32[6912,512]{1,0:T(8,128)} %get-tuple-element.272, f32[6912,256]{1,0:T(8,128)S(1)} %bitcast.28, s32[256]{0:T(256)S(1)} %bitcast.36, s32[512]{0:T(512)S(1)} %iota_add_fusion.5), kind=kOutput, calls=%fused_computation.2.clone.1 | convolution fusion | flops 10876092416 | bytes 35392512 | tf_op jit(solution)/shard_map/while/body/dot_general | solution.py:53
  109.6 16.8 %convolution_add_fusion.2 = f32[6912,512]{1,0:T(8,128)} fusion(f32[6912,512]{1,0:T(8,128)} %get-tuple-element.272, f32[6912,256]{1,0:T(8,128)S(1)} %bitcast.28, s32[256]{0:T(256)S(1)} %bitcast.36, s32[512]{0:T(512)S(1)} %iota_add_fusion.5), kind=kOutput, calls=%fused_computation.2.clone.1 | convolution fusion | flops 10876092416 | bytes 35392512 | tf_op jit(solution)/shard_map/while/body/dot_general | solution.py:53
  126.4 4.9 %fusion.32 = (f32[3,2048,128]{2,1,0:T(8,128)S(1)}, f32[3,2048,128]{2,1,0:T(8,128)}) fusion(f32[3,2304,512]{2,1,0:T(8,128)} %bitcast.29), kind=kLoop, calls=%fused_computation.53 | loop fusion | bytes 12582912 | tf_op jit(solution)/shard_map/slice | solution.py:99
  131.3 41.8 %collective-permute-start.2 = (f32[3,2048,128]{2,1,0:T(8,128)}, f32[3,2048,128]{2,1,0:T(8,128)}, u32[]{:S(2)}, u32[]{:S(2)}) collective-permute-start(f32[3,2048,128]{2,1,0:T(8,128)} %get-tuple-element.190), channel_id=1, source_target_pairs={{0,3},{1,0},{2,1},{3,2},{4,7},{5,4},{6,5},{7,6},{8,11},{9,8},{10,9... | collective-permute-start | bytes 9437192 | tf_op jit(solution)/shard_map/ppermute | solution.py:25
  173.1 2.1 fusion.33
  176.5 4.6 %collective-permute-start.1 = (f32[3,128,256]{2,1,0:T(8,128)}, f32[3,128,256]{2,1,0:T(8,128)S(1)}, u32[]{:S(2)}, u32[]{:S(2)}) collective-permute-start(f32[3,128,256]{2,1,0:T(8,128)} %get-tuple-element.191), channel_id=1, source_target_pairs={{0,4},{4,8},{8,12},{12,16},{16,20},{20,24},{24,28},{1,5},{5,9},{9,... | collective-permute-start | bytes 1179656 | tf_op jit(solution)/shard_map/ppermute | solution.py:20
  181.0 2.2 fusion.31
  187.0 87.8 %psum.7 = f32[]{:T(128)} all-reduce(f32[]{:T(128)S(6)} %convert_element_type.23), channel_id=1, replica_groups=mesh['gy'=8,'gz'=4] {'gy','gz'}, use_global_device_ids=true, to_apply=%region_0.0 | all-reduce | flops 1 | bytes 8 | tf_op jit(solution)/shard_map/psum | solution.py:78
  274.9 5.9 %slice.329 = f32[3,2048,256]{2,1,0:T(8,128)} slice(f32[3,2304,512]{2,1,0:T(8,128)} %bitcast.32), slice={[0:3], [128:2176], [128:384]} | slice | bytes 12582912 | tf_op jit(solution)/shard_map/slice | solution.py:108
  282.9 4.4 %collective-permute-start.6 = (f32[3,128,128]{2,1,0:T(8,128)}, f32[3,128,128]{2,1,0:T(8,128)S(1)}, u32[]{:S(2)}, u32[]{:S(2)}) collective-permute-start(f32[3,128,128]{2,1,0:T(8,128)} %get-tuple-element.187), channel_id=1, source_target_pairs={{0,4},{4,8},{8,12},{12,16},{16,20},{20,24},{24,28},{1,5},{5,9},{9,... | collective-permute-start | bytes 589832 | tf_op jit(solution)/shard_map/ppermute | solution.py:20
  287.4 1.9 fusion.26
  290.6 5.2 %collective-permute-start.10 = (f32[3,128,128]{2,1,0:T(8,128)}, f32[3,128,128]{2,1,0:T(8,128)}, u32[]{:S(2)}, u32[]{:S(2)}) collective-permute-start(f32[3,128,128]{2,1,0:T(8,128)} %get-tuple-element.185), channel_id=1, source_target_pairs={{0,4},{4,8},{8,12},{12,16},{16,20},{20,24},{24,28},{1,5},{5,9},{9,... | collective-permute-start | bytes 589832 | tf_op jit(solution)/shard_map/ppermute | solution.py:20
  301.0 4.8 %fusion.23 = f32[3,2048,256]{2,1,0:T(8,128)} fusion(f32[3,2048,256]{2,1,0:T(8,128)} %fusion.25, f32[3,2048,128]{2,1,0:T(8,128)} %collective-permute-done.2), kind=kLoop, calls=%fused_computation.32 | loop fusion | flops 786432 | bytes 9437184 | tf_op jit(solution)/shard_map/scatter-add | solution.py:111
  305.9 5.0 %fusion.22 = f32[3,2048,256]{2,1,0:T(8,128)} fusion(f32[3,2048,256]{2,1,0:T(8,128)} %fusion.23, f32[3,2048,128]{2,1,0:T(8,128)} %collective-permute-done.3), kind=kLoop, calls=%fused_computation.30 | loop fusion | flops 786432 | bytes 9437184 | tf_op jit(solution)/shard_map/scatter-add | solution.py:112
  312.5 3.0 add_select_fusion
  315.5 4.0 %scatter-add.35 = f32[3,2048,256]{2,1,0:T(8,128)} dynamic-update-slice(f32[3,2048,256]{2,1,0:T(8,128)} %fusion.29, f32[3,128,128]{2,1,0:T(8,128)S(1)} %add_select_fusion, s32[]{:T(128)} %constant.270.clone.1, s32[]{:T(128)} %bitcast.4, s32[]{:T(128)} %bitcast.5) | dynamic-update-slice | bytes 393220 | tf_op jit(solution)/shard_map/scatter-add | solution.py:114
  322.8 4.6 %slice_multiply_fusion.1 = (f32[1,2048,256]{2,1,0:T(8,128)S(1)}, f32[1,2048,256]{2,1,0:T(8,128)S(1)}, f32[1,2048,256]{2,1,0:T(8,128)S(1)}) fusion(f32[3,2048,256]{2,1,0:T(8,128)} %fusion.27, f32[2048]{0:T(1024)S(1)} %bitcast.39, f32[2048]{0:T(1024)S(1)} %bitcast.40, f32[2048]{0:T(1024)S(1)} %bitcast.43, f32[2048]{0:T(1024)S(1)} %bitcast.44, ...), kind=kLoop, calls=%fused_computation.36 | loop fusion | flops 4718592 | bytes 12632064 | tf_op jit(solution)/shard_map/mul | solution.py:66
  327.5 3.1 fusion.21
  (91 shorter events, 35.8 us)
Async XLA Ops:
  126.4 58.2 %copy-start.4 = (f32[3,2048]{1,0:T(4,128)S(1)}, f32[3,2048]{1,0:T(4,128)}, u32[]{:S(2)}) copy-start(f32[3,2048]{1,0:T(4,128)} %param.27) | copy-start | bytes 73732
  126.4 58.8 %copy-start.5 = (f32[3,2048]{1,0:T(4,128)S(1)}, f32[3,2048]{1,0:T(4,128)}, u32[]{:S(2)}) copy-start(f32[3,2048]{1,0:T(4,128)} %param.28) | copy-start | bytes 73732
  131.3 168.0 %collective-permute-start.2 = (f32[3,2048,128]{2,1,0:T(8,128)}, f32[3,2048,128]{2,1,0:T(8,128)}, u32[]{:S(2)}, u32[]{:S(2)}) collective-permute-start(f32[3,2048,128]{2,1,0:T(8,128)} %get-tuple-element.190), channel_id=1, source_target_pairs={{0,3},{1,0},{2,1},{3,2},{4,7},{5,4},{6,5},{7,6},{8,11},{9,8},{10,9... | collective-permute-start | bytes 9437192 | tf_op jit(solution)/shard_map/ppermute | solution.py:25
  173.1 132.8 %collective-permute-start.3 = (f32[3,2048,128]{2,1,0:T(8,128)S(1)}, f32[3,2048,128]{2,1,0:T(8,128)}, u32[]{:S(2)}, u32[]{:S(2)}) collective-permute-start(f32[3,2048,128]{2,1,0:T(8,128)S(1)} %get-tuple-element.189), channel_id=1, source_target_pairs={{0,1},{1,2},{2,3},{3,0},{4,5},{5,6},{6,7},{7,4},{8,9},{9,10},{10,1... | collective-permute-start | bytes 9437192 | tf_op jit(solution)/shard_map/ppermute | solution.py:25
  175.2 107.8 %collective-permute-start = (f32[3,128,256]{2,1,0:T(8,128)}, f32[3,128,256]{2,1,0:T(8,128)}, u32[]{:S(2)}, u32[]{:S(2)}) collective-permute-start(f32[3,128,256]{2,1,0:T(8,128)} %get-tuple-element.192), channel_id=1, source_target_pairs={{4,0},{8,4},{12,8},{16,12},{20,16},{24,20},{28,24},{5,1},{9,5},{13... | collective-permute-start | bytes 1179656 | tf_op jit(solution)/shard_map/ppermute | solution.py:20
  176.5 114.1 %collective-permute-start.1 = (f32[3,128,256]{2,1,0:T(8,128)}, f32[3,128,256]{2,1,0:T(8,128)S(1)}, u32[]{:S(2)}, u32[]{:S(2)}) collective-permute-start(f32[3,128,256]{2,1,0:T(8,128)} %get-tuple-element.191), channel_id=1, source_target_pairs={{0,4},{4,8},{8,12},{12,16},{16,20},{20,24},{24,28},{1,5},{5,9},{9,... | collective-permute-start | bytes 1179656 | tf_op jit(solution)/shard_map/ppermute | solution.py:20
  183.3 106.0 %collective-permute-start.4 = (f32[3,128,128]{2,1,0:T(8,128)}, f32[3,128,128]{2,1,0:T(8,128)}, u32[]{:S(2)}, u32[]{:S(2)}) collective-permute-start(f32[3,128,128]{2,1,0:T(8,128)} %get-tuple-element.188), channel_id=1, source_target_pairs={{4,0},{8,4},{12,8},{16,12},{20,16},{24,20},{28,24},{5,1},{9,5},{13... | collective-permute-start | bytes 589832 | tf_op jit(solution)/shard_map/ppermute | solution.py:20
  185.8 0.6 copy-start.6
  282.9 14.7 %collective-permute-start.6 = (f32[3,128,128]{2,1,0:T(8,128)}, f32[3,128,128]{2,1,0:T(8,128)S(1)}, u32[]{:S(2)}, u32[]{:S(2)}) collective-permute-start(f32[3,128,128]{2,1,0:T(8,128)} %get-tuple-element.187), channel_id=1, source_target_pairs={{0,4},{4,8},{8,12},{12,16},{16,20},{20,24},{24,28},{1,5},{5,9},{9,... | collective-permute-start | bytes 589832 | tf_op jit(solution)/shard_map/ppermute | solution.py:20
  289.3 8.3 %collective-permute-start.8 = (f32[3,128,128]{2,1,0:T(8,128)}, f32[3,128,128]{2,1,0:T(8,128)}, u32[]{:S(2)}, u32[]{:S(2)}) collective-permute-start(f32[3,128,128]{2,1,0:T(8,128)} %get-tuple-element.186), channel_id=1, source_target_pairs={{4,0},{8,4},{12,8},{16,12},{20,16},{24,20},{28,24},{5,1},{9,5},{13... | collective-permute-start | bytes 589832 | tf_op jit(solution)/shard_map/ppermute | solution.py:20
  290.6 8.7 %collective-permute-start.10 = (f32[3,128,128]{2,1,0:T(8,128)}, f32[3,128,128]{2,1,0:T(8,128)}, u32[]{:S(2)}, u32[]{:S(2)}) collective-permute-start(f32[3,128,128]{2,1,0:T(8,128)} %get-tuple-element.185), channel_id=1, source_target_pairs={{0,4},{4,8},{8,12},{12,16},{16,20},{20,24},{24,28},{1,5},{5,9},{9,... | collective-permute-start | bytes 589832 | tf_op jit(solution)/shard_map/ppermute | solution.py:20
  297.6 13.2 %collective-permute-start.5 = (f32[3,128,128]{2,1,0:T(8,128)}, f32[3,128,128]{2,1,0:T(8,128)S(1)}, u32[]{:S(2)}, u32[]{:S(2)}) collective-permute-start(f32[3,128,128]{2,1,0:T(8,128)} %collective-permute-done.4), channel_id=1, source_target_pairs={{0,3},{1,0},{2,1},{3,2},{4,7},{5,4},{6,5},{7,6},{8,11},{9,8},{10,9... | collective-permute-start | bytes 589832 | tf_op jit(solution)/shard_map/ppermute | solution.py:25
  297.6 14.9 %collective-permute-start.7 = (f32[3,128,128]{2,1,0:T(8,128)S(1)}, f32[3,128,128]{2,1,0:T(8,128)S(1)}, u32[]{:S(2)}, u32[]{:S(2)}) collective-permute-start(f32[3,128,128]{2,1,0:T(8,128)S(1)} %collective-permute-done.6), channel_id=1, source_target_pairs={{0,3},{1,0},{2,1},{3,2},{4,7},{5,4},{6,5},{7,6},{8,11},{9,8},{10,9... | collective-permute-start | bytes 589832 | tf_op jit(solution)/shard_map/ppermute | solution.py:25
  299.3 20.2 %collective-permute-start.9 = (f32[3,128,128]{2,1,0:T(8,128)}, f32[3,128,128]{2,1,0:T(8,128)S(1)}, u32[]{:S(2)}, u32[]{:S(2)}) collective-permute-start(f32[3,128,128]{2,1,0:T(8,128)} %collective-permute-done.8), channel_id=1, source_target_pairs={{0,1},{1,2},{2,3},{3,0},{4,5},{5,6},{6,7},{7,4},{8,9},{9,10},{10,1... | collective-permute-start | bytes 589832 | tf_op jit(solution)/shard_map/ppermute | solution.py:25
  299.3 21.8 %collective-permute-start.11 = (f32[3,128,128]{2,1,0:T(8,128)}, f32[3,128,128]{2,1,0:T(8,128)S(1)}, u32[]{:S(2)}, u32[]{:S(2)}) collective-permute-start(f32[3,128,128]{2,1,0:T(8,128)} %collective-permute-done.10), channel_id=1, source_target_pairs={{0,1},{1,2},{2,3},{3,0},{4,5},{5,6},{6,7},{7,4},{8,9},{9,10},{10,1... | collective-permute-start | bytes 589832 | tf_op jit(solution)/shard_map/ppermute | solution.py:25
  305.8 16.9 %copy-start = (f32[1,2048]{1,0:T(1,128)S(1)}, f32[1,2048]{1,0:T(1,128)}, u32[]{:S(2)}) copy-start(f32[1,2048]{1,0:T(1,128)} %get-tuple-element.198) | copy-start | bytes 24580
  305.8 16.9 %copy-start.1 = (f32[1,2048]{1,0:T(1,128)S(1)}, f32[1,2048]{1,0:T(1,128)}, u32[]{:S(2)}) copy-start(f32[1,2048]{1,0:T(1,128)} %get-tuple-element.199) | copy-start | bytes 24580
  305.9 16.9 %copy-start.2 = (f32[1,2048]{1,0:T(1,128)S(1)}, f32[1,2048]{1,0:T(1,128)}, u32[]{:S(2)}) copy-start(f32[1,2048]{1,0:T(1,128)} %get-tuple-element.200) | copy-start | bytes 24580
  305.9 16.9 %copy-start.3 = (f32[1,2048]{1,0:T(1,128)S(1)}, f32[1,2048]{1,0:T(1,128)}, u32[]{:S(2)}) copy-start(f32[1,2048]{1,0:T(1,128)} %get-tuple-element.201) | copy-start | bytes 24580
  305.9 21.6 %slice-start = ((s8[6291456]{0:T(1024)(128)(4,1)}), s8[2097152]{0:T(1024)(128)(4,1)S(1)}, s32[]{:S(2)}) async-start(s8[6291456]{0:T(1024)(128)(4,1)} %bitcast.34), calls=%async_computation | async-start | bytes 4194304
  322.8 4.7 %slice-start.1 = ((s8[6291456]{0:T(1024)(128)(4,1)}), s8[4194304]{0:T(1024)(128)(4,1)S(1)}, s32[]{:S(2)}) async-start(s8[6291456]{0:T(1024)(128)(4,1)} %bitcast.34), calls=%async_computation.1 | async-start | bytes 8388608
where the time goes:
time: 331 us
  matrix products  101 us (31%)
  blocking collectives  87.8 us (27%)
  starting transfers between devices  61.7 us (19%)
  other arithmetic  42.7 us (13%)
  local copies, waits for them, and re-layouts  34.3 us (10%)
    dot_general x6, matrix products, add_block(): lax.dot_general(signed, span_profile, (((1,), (1,)), ((), ())), precision...  101 us
    psum x1, blocking collectives, body(): eddy_total = lax.psum(live_count.astype(jnp.float32), ('gy', 'gz'))  87.8 us
    ppermute x6, starting transfers between devices, passed_along_2(): lax.ppermute(value, axis, [(i, (i + by) % peers) for i in range(peers)])  43.7 us
    ppermute x6, starting transfers between devices, passed_along(): return lax.ppermute(value, axis, pairs)  18.1 us
    broadcast_in_dim x1, local copies, waits for them, and re-layouts, tile_field(): initial = jnp.zeros((3 * ext_rows, ext_cols), jnp.float32)  6.84 us
  transfers between devices with their start and end apart: 12, of which 1 were waited for; matrix products, arithmetic and copies ran while one was open for 11% of the time, Pallas kernels for 0%

commit v1 on v0

v1 whole, which is shorter than its diff:
```python
import functools

import jax
import jax.numpy as jnp
from jax import lax
from jax.experimental import pallas as pl
from jax.experimental.pallas import tpu as pltpu
from jax.sharding import PartitionSpec as P


HALF = 128
ROWS = 512
CHUNK = 1024
KNOWN, COUNT = 5, 6


def pairs_near(size):
    return [(i, i ^ 1) for i in range(size)]


def pairs_far(size):
    return [(i, (i + 1 if i % 2 else i - 1) % size) for i in range(size)]


def pairs_inner(size):
    return [(i, i + 1 if i % 2 else i - 1) for i in range(1, size - 1)]


def pairs_over(size, by):
    return [(i, i ^ by) for i in range(size)]


def pairs_skip(size):
    skips, by = [], 4
    while by < size:
        skips.append(pairs_over(size, by))
        by *= 2
    return skips


def covers(rounds, size):
    known = [{i} for i in range(size)]
    for pairs in rounds:
        known = [known[i] | known[dict(pairs)[i]] for i in range(size)]
    return size > 2 and all(len(k) == size for k in known)


def whole(values):
    return values.astype(jnp.float32).astype(jnp.bfloat16)


def cells_of(nrows, ncols):
    cells = whole(lax.broadcasted_iota(jnp.int32, (nrows, HALF), 0) - HALF)
    return jnp.concatenate([cells] * (ncols // HALF), axis=1)


def tent(cells, places, origin):
    near = whole(jnp.clip(places - (origin + HALF), -2 * HALF, 2 * HALF))
    return jnp.maximum(HALF - jnp.abs(cells - near), 0).astype(jnp.bfloat16)


def wall_profiles(tile, row, nrows):
    step = min(nrows, 2 * HALF)
    cells = cells_of(step, tile.shape[1])
    return jnp.concatenate([tent(cells, tile[0:1, :], row + r) for r in range(0, nrows, step)], axis=0)


def chunks_of(slots):
    return (slots + CHUNK - 1) // CHUNK


def at_chunk(k):
    return pl.ds(pl.multiple_of(k * CHUNK, CHUNK), CHUNK)


def contract(a, b):
    return lax.dot_general(a, b, (((1,), (1,)), ((), ())), preferred_element_type=jnp.float32)


def fill_span(tile_ref, span_ref, slots, column):
    ncols = span_ref.shape[0] // 3

    def fill_chunk(k, carry):
        tile = tile_ref[:, at_chunk(k)]
        span = tent(cells_of(ncols, CHUNK), tile[1:2, :], column)
        signs = whole(tile[2:5, :])
        for c in range(3):
            span_ref[c * ncols : (c + 1) * ncols, at_chunk(k)] = span * signs[c : c + 1, :]
        return carry

    lax.fori_loop(0, chunks_of(slots), fill_chunk, 0)


def add_tile(out, tile_ref, span_ref, slots, row, column):
    ncols = span_ref.shape[0] // 3

    def add_chunk(k, carry):
        part = contract(wall_profiles(tile_ref[:, at_chunk(k)], row, ROWS), span_ref[:, at_chunk(k)])
        for c in range(3):
            out[c, :, pl.ds(column, ncols)] += part[:, c * ncols : (c + 1) * ncols]
        return carry

    lax.fori_loop(0, chunks_of(slots), add_chunk, 0)


def add_edge(out, tiles_ref, row, at_row, even_z):
    cols = out.shape[-1]

    def add(t, carry):
        tile = tiles_ref[t]
        column = jnp.where(even_z == 1, (1 - t) * cols, (t - 1) * cols)
        wall = wall_profiles(tile, row, HALF)
        signs = whole(tile[2:5, :])
        part = contract(
            jnp.concatenate([wall * signs[c : c + 1, :] for c in range(3)], axis=0),
            tent(cells_of(cols, tile.shape[1]), tile[1:2, :], column),
        )
        for c in range(3):
            out[c, pl.ds(at_row, HALF), :] += part[c * HALF : (c + 1) * HALF, :]
        return carry

    lax.fori_loop(0, 3, add, 0)


def edge_of(below, rows):
    return jnp.where(below == 1, -HALF, rows), pl.multiple_of(below * (ROWS - HALF), HALF)


def own_kernel(heads, tile, *refs, first):
    out, span = refs[-2:]
    block = pl.program_id(0)

    @pl.when(block == 0)
    def _():
        fill_span(tile, span, heads[COUNT, 0], 0)

    out[...] = jnp.zeros_like(out)
    add_tile(out, tile, span, heads[COUNT, 0], first + block * ROWS, 0)


def side_of(side, ncols):
    return jnp.where(side == 1, -ncols, 2 * ncols), pl.multiple_of(side * ncols, ncols)


def side_kernel(heads, own, tile, field, out, span):
    block = pl.program_id(0)
    ncols = span.shape[0] // 3
    origin, column = side_of(1 - own[COUNT, 2] % 2, ncols)

    @pl.when(block == 0)
    def _():
        fill_span(tile, span, heads[COUNT, 0], origin)

    out[...] = field[...]
    add_tile(out, tile, span, heads[COUNT, 0], block * ROWS, column)


def edge_kernel(own, tiles, out, *, rows):
    row, _ = edge_of(1 - own[COUNT, 1] % 2, rows)
    out[...] = jnp.zeros_like(out)
    add_edge(out, tiles, row, 0, 1 - own[COUNT, 2] % 2)


def last_kernel(heads, own, side, far, known, edge, diag, shear, mean, field, out, span, acc, *, rows, tiles_y, scale):
    block = pl.program_id(0)
    nblocks = rows // ROWS
    ncols = span.shape[0] // 3
    at_y, odd_z = own[COUNT, 1], own[COUNT, 2] % 2
    odd_y = at_y % 2
    origin, column = side_of(odd_z, ncols)
    acc[...] = field[...]

    @pl.when(block == 0)
    def _():
        fill_span(side, span, heads[COUNT, 0], origin)

    add_tile(acc, side, span, heads[COUNT, 0], block * ROWS, column)

    @pl.when(block == (1 - odd_y) * (nblocks - 1))
    def _():
        _, at_row = edge_of(1 - odd_y, rows)
        acc[:, pl.ds(at_row, HALF), :] += edge[...]

    @pl.when((block == odd_y * (nblocks - 1)) & (at_y > 0) & (at_y < tiles_y - 1))
    def _():
        row, at_row = edge_of(odd_y, rows)
        add_edge(acc, far, row, at_row, 1 - odd_z)

    total = jnp.sum(known[...].astype(jnp.float32), axis=1, keepdims=True)
    amplitude = jnp.sqrt(scale / total) * (1.5 / (HALF * HALF))
    factors = jnp.concatenate([diag[...], shear[...], jnp.zeros((2, ROWS), jnp.float32)], axis=0) * amplitude
    factors = factors.T
    a0, a1, a2 = (factors[:, k : k + 1] for k in range(3))
    b0, b1, b2 = (factors[:, 3 + k : 4 + k] for k in range(3))
    out[0] = mean[0] + a0 * acc[0]
    out[1] = mean[1] + (b0 * acc[0] + a1 * acc[1])
    out[2] = mean[2] + (b1 * acc[0] + b2 * acc[1] + a2 * acc[2])


def with_known(tile, known):
    return jnp.where(jnp.arange(tile.shape[0])[:, None] == KNOWN, known[None], tile)


def packed(places, signs, count, at_y, at_z, number):
    slots = places.shape[-1]
    slot = jnp.arange(slots, dtype=jnp.int32)[None]
    row = jnp.arange(8, dtype=jnp.int32)[:, None]
    signs = jnp.where(slot < count, signs, 0)
    known = jnp.where((row == KNOWN) & (slot == number), count, 0)
    place = jnp.where(slot == 0, count, jnp.where(slot == 1, at_y, at_z))
    rest = known + jnp.where(row == COUNT, place, 0)
    return jnp.pad(places, ((0, 6), (0, 0))) + jnp.pad(signs, ((2, 3), (0, 0))) + rest


def body(eddy_cells, eddy_signs, eddy_counts, stress_diag, stress_shear, mean_flow):
    slots = eddy_cells.shape[-1]
    _, rows, cols = mean_flow.shape
    tiles_y, tiles_z = lax.axis_size("gy"), lax.axis_size("gz")
    at_y, at_z = lax.axis_index("gy"), lax.axis_index("gz")
    assert cols == 2 * HALF and rows % (2 * ROWS) == 0 and tiles_y * tiles_z <= slots and slots % CHUNK == 0
    assert covers([pairs_near(tiles_z), pairs_far(tiles_z)] + pairs_skip(tiles_z), tiles_z)
    assert covers(pairs_skip(tiles_y) + [pairs_near(tiles_y), pairs_over(tiles_y, 2)], tiles_y)

    vmem = pl.BlockSpec(memory_space=pltpu.VMEM)
    anywhere = pl.BlockSpec(memory_space=pl.ANY)
    heads = pl.BlockSpec((8, HALF), lambda i: (0, 0), memory_space=pltpu.SMEM)
    field_block = pl.BlockSpec((3, ROWS, cols), lambda i: (0, i, 0))
    field_shape = jax.ShapeDtypeStruct((3, rows, cols), jnp.float32)
    own_span = pltpu.VMEM((3 * cols, slots), jnp.bfloat16)
    side_span = pltpu.VMEM((3 * HALF, slots), jnp.bfloat16)
    macs = 3 * rows * cols * slots

    def cost(part, moved):
        return pl.CostEstimate(flops=int(2 * macs * part), transcendentals=0, bytes_accessed=int(4 * moved * 3 * rows * cols))

    def own_part(first, tile, field=None):
        return pl.pallas_call(
            functools.partial(own_kernel, first=first),
            grid=(rows // ROWS // 2,),
            in_specs=[heads, vmem] + ([] if field is None else [anywhere]),
            out_specs=pl.BlockSpec((3, ROWS, cols), lambda i: (0, i + first // ROWS, 0)),
            out_shape=field_shape,
            scratch_shapes=[own_span],
            input_output_aliases={} if field is None else {2: 0},
            cost_estimate=cost(0.5, 0.5),
        )(tile, tile, *([] if field is None else [field]))

    anchor = jnp.stack([at_y * rows, at_z * cols]).astype(jnp.int32)
    places = eddy_cells.reshape(2, slots) - anchor[:, None]
    own = packed(places, eddy_signs.reshape(3, slots), eddy_counts.reshape(()), at_y, at_z, at_y * tiles_z + at_z)

    near_z = lax.ppermute(own, "gz", pairs_near(tiles_z))
    known = jnp.maximum(own[KNOWN], near_z[KNOWN])
    far_z = lax.ppermute(with_known(own, known), "gz", pairs_far(tiles_z))
    field = own_part(0, own)
    known = jnp.maximum(known, far_z[KNOWN])
    for pairs in pairs_skip(tiles_z):
        known = jnp.maximum(known, lax.ppermute(known, "gz", pairs))
    for pairs in pairs_skip(tiles_y):
        known = jnp.maximum(known, lax.ppermute(known, "gy", pairs))
    field = own_part(rows // 2, own, field)
    row_of_tiles = jnp.stack([far_z, with_known(own, known), near_z])
    near_y = lax.ppermute(row_of_tiles, "gy", pairs_near(tiles_y))
    far_y = lax.ppermute(row_of_tiles, "gy", pairs_inner(tiles_y))
    field = pl.pallas_call(
        side_kernel,
        grid=(rows // ROWS,),
        in_specs=[heads, heads, vmem, field_block],
        out_specs=field_block,
        out_shape=field_shape,
        scratch_shapes=[side_span],
        input_output_aliases={3: 0},
        cost_estimate=cost(0.7, 2.0),
    )(near_z, own, near_z, field)
    known = jnp.maximum(known, near_y[1, KNOWN])
    over = lax.ppermute(known, "gy", pairs_over(tiles_y, 2))
    known = jnp.maximum(known, over)[None]
    edge = pl.pallas_call(
        functools.partial(edge_kernel, rows=rows),
        grid=(1,),
        in_specs=[heads, vmem],
        out_specs=vmem,
        out_shape=jax.ShapeDtypeStruct((3, HALF, cols), jnp.float32),
        cost_estimate=cost(0.2, 0.1),
    )(own, near_y)

    stress_block = pl.BlockSpec((3, ROWS), lambda i: (0, i))
    scale = rows * tiles_y * (cols * tiles_z) / (HALF * HALF)
    return pl.pallas_call(
        functools.partial(last_kernel, rows=rows, tiles_y=tiles_y, scale=scale),
        grid=(rows // ROWS,),
        in_specs=[heads, heads, vmem, vmem, vmem, vmem, stress_block, stress_block, field_block, field_block],
        out_specs=field_block,
        out_shape=field_shape,
        scratch_shapes=[side_span, pltpu.VMEM((3, ROWS, cols), jnp.float32)],
        cost_estimate=cost(0.5, 3.0),
    )(far_z, own, far_z, far_y, known, edge, stress_diag, stress_shear, mean_flow, field)


def solution(mesh):
    in_specs = (
        P("gy", "gz", None, None),
        P("gy", "gz", None, None),
        P("gy", "gz"),
        P(None, "gy"),
        P(None, "gy"),
        P(None, "gy", "gz"),
    )

    return jax.shard_map(body, mesh=mesh, in_specs=in_specs, out_specs=P(None, "gy", "gz"), check_vma=False)
```

time: 331 us -> 56.2 us (0.17)
  the two profiles are of different devices: /device:TPU:0 before, /device:TPU:1 now
where the time goes in v1:
time: 56.2 us; the launch traced here: 55.8 us
  Pallas kernels  40.7 us (72%)
  starting transfers between devices  9.77 us (17%)
  other arithmetic  2.57 us (5%)
  waiting for transfers between devices  1.25 us (2%)
  between operations  0.78 us (1%)
  local copies, waits for them, and re-layouts  0.72 us (1%)
    pallas_call x2, Pallas kernels, own_part(): pl.pallas_call(functools.partial(own_kernel, first=first), grid=(rows //...  13.7 us
    pallas_call x1, Pallas kernels, body(): pl.pallas_call(functools.partial(last_kernel, rows=rows, tiles_y=tiles_y,...  13.6 us
    pallas_call x1, Pallas kernels, body(): pl.pallas_call(side_kernel, grid=(rows // ROWS,), in_specs=[heads, heads,...  9.73 us
    ppermute x1, starting transfers between devices, body(): over = lax.ppermute(known, 'gy', pairs_over(tiles_y, 2))  3.92 us
    pallas_call x1, Pallas kernels, body(): pl.pallas_call(functools.partial(edge_kernel, rows=rows), grid=(1,), in_s...  3.62 us
    ppermute x1, starting transfers between devices, body(): far_z = lax.ppermute(with_known(own, known), 'gz', pairs_far(tiles_z))  2.65 us
    ppermute x1, starting transfers between devices, body(): known = jnp.maximum(known, lax.ppermute(known, 'gy', pairs))  2.37 us
    ppermute x1, waiting for transfers between devices, body(): near_z = lax.ppermute(own, 'gz', pairs_near(tiles_z))  1.24 us
  transfers between devices with their start and end apart: 6, of which 1 were waited for; matrix products, arithmetic and copies ran while one was open for 1% of the time, Pallas kernels for 48%

profile of v1, /device:TPU:1, one launch (start us, length us, event | category | flops | bytes accessed | tf_op | source)
XLA Modules:
  0.0 55.8 jit_solution(17498184892149498554)
XLA Ops:
  0.7 0.1 pad_add_fusion.1
  0.8 0.8 %bitcast_subtract_fusion = s32[2,2048]{1,0:T(2,128)S(1)} fusion(s32[1,1,2,2048]{3,2,1,0:T(2,128)} %param.6, s32[2]{0:T(128)S(1)} %pad_add_fusion.1), kind=kLoop, calls=%fused_computation.5 | loop fusion | flops 4096 | bytes 32776 | tf_op jit(solution)/shard_map/sub | solution.py:249
  1.6 0.8 %bitcast_select_fusion = s32[3,2048]{1,0:T(4,128)S(1)} fusion(s32[1,1,3,2048]{3,1,2,0:T(1,128)} %param.7, pred[2048]{0:T(1024)(128)(4,1)S(1)} %iota_compare_fusion.3), kind=kLoop, calls=%fused_computation.3 | loop fusion | flops 6144 | bytes 51200 | tf_op jit(solution)/shard_map/jit(_where)/select_n | solution.py:208
  2.3 0.1 add_add_fusion.own.heads.tile
  2.4 0.1 collective-permute-start
  2.5 1.2 %collective-permute-done.heads.tile = s32[8,2048]{1,0:T(8,128)S(1)} collective-permute-done((s32[8,2048]{1,0:T(8,128)S(1)}, s32[8,2048]{1,0:T(8,128)S(1)}, u32[]{:S(2)}, u32[]{:S(2)}) %collective-permute-start) | collective-permute-done | bytes 65568 | tf_op jit(solution)/shard_map/ppermute | solution.py:252
  3.8 0.1 broadcast_select_fusion
  3.9 2.7 %collective-permute-start.1 = (s32[8,2048]{1,0:T(8,128)S(1)}, s32[8,2048]{1,0:T(8,128)S(1)}, u32[]{:S(2)}, u32[]{:S(2)}) collective-permute-start(s32[8,2048]{1,0:T(8,128)S(1)} %broadcast_select_fusion), channel_id=1, source_target_pairs={{0,3},{1,2},{2,1},{3,0},{4,7},{5,6},{6,5},{7,4},{8,11},{9,10},{10,... | collective-permute-start | bytes 196616 | tf_op jit(solution)/shard_map/ppermute | solution.py:254
  6.5 6.9 %shard_map.65.refs_0_ = f32[3,2048,256]{2,1,0:T(8,128)} custom-call(s32[8,2048]{1,0:T(8,128)} %copy-done, s32[8,2048]{1,0:T(8,128)} %copy-done), custom_call_target="tpu_custom_call" | custom-call | flops 3221225472 | bytes 3145728 | tf_op jit(solution)/shard_map/pallas_call | solution.py:237
  13.4 0.0 collective-permute-done.1.heads.side
  13.4 2.4 %collective-permute-start.2 = (s32[2048]{0:T(1024)S(1)}, s32[2048]{0:T(1024)S(1)}, u32[]{:S(2)}, u32[]{:S(2)}) collective-permute-start(s32[2048]{0:T(1024)S(1)} %bitcast.24), channel_id=1, source_target_pairs={{0,16},{4,20},{8,24},{12,28},{16,0},{20,4},{24,8},{28,12},{1,17},{... | collective-permute-start | bytes 24584 | tf_op jit(solution)/shard_map/ppermute | solution.py:260
  15.8 6.8 %shard_map.66.field = f32[3,2048,256]{2,1,0:T(8,128)} custom-call(s32[8,2048]{1,0:T(8,128)} %copy-done, s32[8,2048]{1,0:T(8,128)} %copy-done, f32[3,2048,256]{2,1,0:T(8,128)} %shard_map.65.refs_0_), custom_call_target="tpu_custom_call", output_to_operand_aliasing={{}: (2, {})} | custom-call | flops 3221225472 | bytes 3145728 | tf_op jit(solution)/shard_map/pallas_call | solution.py:237
  22.6 0.0 collective-permute-done.2
  22.6 0.1 select_bitcast_fusion
  22.8 0.1 collective-permute-start.4
  22.9 0.7 %collective-permute-start.3 = (s32[3,8,2048]{2,1,0:T(8,128)S(1)}, s32[3,8,2048]{2,1,0:T(8,128)S(1)}, u32[]{:S(2)}, u32[]{:S(2)}) collective-permute-start(s32[3,8,2048]{2,1,0:T(8,128)S(1)} %pad_add_fusion), channel_id=1, source_target_pairs={{4,8},{8,4},{12,16},{16,12},{20,24},{24,20},{5,9},{9,5},{13,17},{1... | collective-permute-start | bytes 589832 | tf_op jit(solution)/shard_map/ppermute | solution.py:264
  23.5 9.7 %shard_map.67.field = f32[3,2048,256]{2,1,0:T(8,128)} custom-call(s32[8,2048]{1,0:T(8,128)} %copy-done.3, s32[8,2048]{1,0:T(8,128)} %copy-done, s32[8,2048]{1,0:T(8,128)} %copy-done.3, f32[3,2048,256]{2,1,0:T(8,128)} %shard_map.66.field), custom_call_target="tpu_custom_call", output_to_operand_aliasing={{}: (3, {})} | custom-call | flops 4509715456 | bytes 12582912 | tf_op jit(solution)/shard_map/pallas_call | solution.py:265
  33.3 0.0 collective-permute-done.4.tiles
  33.3 3.9 %collective-permute-start.5 = (s32[2048]{0:T(1024)S(1)}, s32[2048]{0:T(1024)S(1)}, u32[]{:S(2)}, u32[]{:S(2)}) collective-permute-start(s32[2048]{0:T(1024)S(1)} %max.24), channel_id=1, source_target_pairs={{0,8},{4,12},{8,0},{12,4},{16,24},{20,28},{24,16},{28,20},{1,9},{5... | collective-permute-start | bytes 24584 | tf_op jit(solution)/shard_map/ppermute | solution.py:276
  37.2 3.6 %shard_map.64.edge = f32[3,128,256]{2,1,0:T(8,128)} custom-call(s32[8,2048]{1,0:T(8,128)} %copy-done, s32[3,8,2048]{2,1,0:T(8,128)} %copy-done.4), custom_call_target="tpu_custom_call" | custom-call | flops 1288490240 | bytes 629145 | tf_op jit(solution)/shard_map/pallas_call | solution.py:278
  40.9 0.0 collective-permute-done.5
  40.9 0.6 %max.25 = s32[2048]{0:T(1024)} maximum(s32[2048]{0:T(1024)S(1)} %max.24, s32[2048]{0:T(1024)S(1)} %collective-permute-done.5) | non-fusion elementwise | flops 2048 | bytes 24576 | tf_op jit(solution)/shard_map/max | solution.py:277
  41.5 0.7 %copy-done.2 = s32[3,8,2048]{2,1,0:T(8,128)} copy-done((s32[3,8,2048]{2,1,0:T(8,128)}, s32[3,8,2048]{2,1,0:T(8,128)S(1)}, u32[]{:S(2)}) %copy-start.2) | copy-done | bytes 196632
  42.1 13.6 %shard_map.68 = f32[3,2048,256]{2,1,0:T(8,128)} custom-call(s32[8,2048]{1,0:T(8,128)} %copy-done.1, s32[8,2048]{1,0:T(8,128)} %copy-done, s32[8,2048]{1,0:T(8,128)} %copy-done.1, s32[3,8,2048]{2,1,0:T(8,128)} %copy-done.2, s32[1,2048]{1,0:T(1,128)} %bitcast.23, f32[3,128,256]{2,1,0:T(8,128)} %shard_map.64.edge, f32[3,2048]{1,0:T(4,128)} %diag.1, ...), custom_call_target="tpu_custom_call" | custom-call | flops 3221225472 | bytes 18874368 | tf_op jit(solution)/shard_map/pallas_call | solution.py:289
  (20 shorter events, 0.1 us)
Async XLA Ops:
  2.4 4.1 %copy-start = (s32[8,2048]{1,0:T(8,128)}, s32[8,2048]{1,0:T(8,128)S(1)}, u32[]{:S(2)}) copy-start(s32[8,2048]{1,0:T(8,128)S(1)} %add_add_fusion.own.heads.tile) | copy-start | bytes 196612
  2.4 1.3 %collective-permute-start = (s32[8,2048]{1,0:T(8,128)S(1)}, s32[8,2048]{1,0:T(8,128)S(1)}, u32[]{:S(2)}, u32[]{:S(2)}) collective-permute-start(s32[8,2048]{1,0:T(8,128)S(1)} %add_add_fusion.own.heads.tile), channel_id=1, source_target_pairs={{0,1},{1,0},{2,3},{3,2},{4,5},{5,4},{6,7},{7,6},{8,9},{9,8},{10,11... | collective-permute-start | bytes 196616 | tf_op jit(solution)/shard_map/ppermute | solution.py:252
  3.8 19.0 %copy-start.3 = (s32[8,2048]{1,0:T(8,128)}, s32[8,2048]{1,0:T(8,128)S(1)}, u32[]{:S(2)}) copy-start(s32[8,2048]{1,0:T(8,128)S(1)} %collective-permute-done.heads.tile) | copy-start | bytes 196612
  3.9 9.5 %collective-permute-start.1 = (s32[8,2048]{1,0:T(8,128)S(1)}, s32[8,2048]{1,0:T(8,128)S(1)}, u32[]{:S(2)}, u32[]{:S(2)}) collective-permute-start(s32[8,2048]{1,0:T(8,128)S(1)} %broadcast_select_fusion), channel_id=1, source_target_pairs={{0,3},{1,2},{2,1},{3,0},{4,7},{5,6},{6,5},{7,4},{8,11},{9,10},{10,... | collective-permute-start | bytes 196616 | tf_op jit(solution)/shard_map/ppermute | solution.py:254
  13.4 9.3 %copy-start.1 = (s32[8,2048]{1,0:T(8,128)}, s32[8,2048]{1,0:T(8,128)S(1)}, u32[]{:S(2)}) copy-start(s32[8,2048]{1,0:T(8,128)S(1)} %collective-permute-done.1.heads.side) | copy-start | bytes 196612
  13.4 9.2 %collective-permute-start.2 = (s32[2048]{0:T(1024)S(1)}, s32[2048]{0:T(1024)S(1)}, u32[]{:S(2)}, u32[]{:S(2)}) collective-permute-start(s32[2048]{0:T(1024)S(1)} %bitcast.24), channel_id=1, source_target_pairs={{0,16},{4,20},{8,24},{12,28},{16,0},{20,4},{24,8},{28,12},{1,17},{... | collective-permute-start | bytes 24584 | tf_op jit(solution)/shard_map/ppermute | solution.py:260
  22.8 10.5 %collective-permute-start.4 = (s32[3,8,2048]{2,1,0:T(8,128)S(1)}, s32[3,8,2048]{2,1,0:T(8,128)S(1)}, u32[]{:S(2)}, u32[]{:S(2)}) collective-permute-start(s32[3,8,2048]{2,1,0:T(8,128)S(1)} %pad_add_fusion), channel_id=1, source_target_pairs={{0,4},{4,0},{8,12},{12,8},{16,20},{20,16},{24,28},{28,24},{1,5},{5... | collective-permute-start | bytes 589832 | tf_op jit(solution)/shard_map/ppermute | solution.py:263
  22.9 18.6 %collective-permute-start.3 = (s32[3,8,2048]{2,1,0:T(8,128)S(1)}, s32[3,8,2048]{2,1,0:T(8,128)S(1)}, u32[]{:S(2)}, u32[]{:S(2)}) collective-permute-start(s32[3,8,2048]{2,1,0:T(8,128)S(1)} %pad_add_fusion), channel_id=1, source_target_pairs={{4,8},{8,4},{12,16},{16,12},{20,24},{24,20},{5,9},{9,5},{13,17},{1... | collective-permute-start | bytes 589832 | tf_op jit(solution)/shard_map/ppermute | solution.py:264
  33.3 4.0 %copy-start.4 = (s32[3,8,2048]{2,1,0:T(8,128)}, s32[3,8,2048]{2,1,0:T(8,128)S(1)}, u32[]{:S(2)}) copy-start(s32[3,8,2048]{2,1,0:T(8,128)S(1)} %collective-permute-done.4.tiles) | copy-start | bytes 589828
  33.3 7.5 %collective-permute-start.5 = (s32[2048]{0:T(1024)S(1)}, s32[2048]{0:T(1024)S(1)}, u32[]{:S(2)}, u32[]{:S(2)}) collective-permute-start(s32[2048]{0:T(1024)S(1)} %max.24), channel_id=1, source_target_pairs={{0,8},{4,12},{8,0},{12,4},{16,24},{20,28},{24,16},{28,20},{1,9},{5... | collective-permute-start | bytes 24584 | tf_op jit(solution)/shard_map/ppermute | solution.py:276
  41.5 0.7 %copy-start.2 = (s32[3,8,2048]{2,1,0:T(8,128)}, s32[3,8,2048]{2,1,0:T(8,128)S(1)}, u32[]{:S(2)}) copy-start(s32[3,8,2048]{2,1,0:T(8,128)S(1)} %collective-permute-done.3.far) | copy-start | bytes 589828

commit v2 on v1

v2 whole, which is shorter than its diff:
```python
import functools

import jax
import jax.numpy as jnp
from jax import lax
from jax.experimental import pallas as pl
from jax.experimental.pallas import tpu as pltpu
from jax.sharding import PartitionSpec as P


HALF = 128
ROWS = 512
LAST_ROWS = 256
WINDOW = 512
EDGE_WINDOW = 256
SORT = 256
KNOWN, HEAD, START = 5, 6, 3


def pairs_near(size):
    return [(i, i ^ 1) for i in range(size)]


def pairs_far(size):
    return [(i, (i + 1 if i % 2 else i - 1) % size) for i in range(size)]


def pairs_inner(size):
    return [(i, i + 1 if i % 2 else i - 1) for i in range(1, size - 1)]


def pairs_over(size, by):
    return [(i, i ^ by) for i in range(size)]


def pairs_skip(size):
    skips, by = [], 4
    while by < size:
        skips.append(pairs_over(size, by))
        by *= 2
    return skips


def covers(rounds, size):
    known = [{i} for i in range(size)]
    for pairs in rounds:
        known = [known[i] | known[dict(pairs)[i]] for i in range(size)]
    return size > 2 and all(len(k) == size for k in known)


def whole(values):
    return values.astype(jnp.float32).astype(jnp.bfloat16)


def cells_of(nrows, ncols):
    cells = whole(lax.broadcasted_iota(jnp.int32, (nrows, HALF), 0) - HALF)
    return jnp.concatenate([cells] * (ncols // HALF), axis=1)


def tent(cells, places, origin):
    near = whole(jnp.clip(places - (origin + HALF), -2 * HALF, 2 * HALF))
    return jnp.maximum(HALF - jnp.abs(cells - near), 0).astype(jnp.bfloat16)


def wall_profiles(tile, row, nrows):
    step = min(nrows, 2 * HALF)
    cells = cells_of(step, tile.shape[1])
    return jnp.concatenate([tent(cells, tile[0:1, :], row + r) for r in range(0, nrows, step)], axis=0)


def contract(a, b):
    return lax.dot_general(a, b, (((1,), (1,)), ((), ())), preferred_element_type=jnp.float32)


def order_kernel(heads, tile, out, *, bands):
    slots = tile.shape[1]
    nbuckets = -(-(2 * bands + 1) // 16) * 16
    places = tile[0:2, :]
    slot = lax.broadcasted_iota(jnp.int32, (1, slots), 1)
    bucket = jnp.where(slot < heads[HEAD, 0], (places[1:2] >> 7) * bands + (places[0:1] >> 7), 2 * bands)
    ids = lax.broadcasted_iota(jnp.int32, (nbuckets, HALF), 0)
    wide_ids = jnp.concatenate([ids] * (slots // HALF), axis=1)
    starts = jnp.sum((bucket < wide_ids).astype(jnp.float32), axis=1, keepdims=True)
    member = jnp.maximum(1 - jnp.abs(whole(wide_ids) - whole(bucket)), 0).astype(jnp.bfloat16)
    upto = lax.broadcasted_iota(jnp.int32, (SORT, SORT), 0) <= lax.broadcasted_iota(jnp.int32, (SORT, SORT), 1)
    pieces = [member[:, k : k + SORT] for k in range(0, slots, SORT)]
    so_far = lax.dot_general(
        jnp.concatenate(pieces, axis=0),
        whole(upto.astype(jnp.int32)),
        (((1,), (0,)), ((), ())),
        preferred_element_type=jnp.float32,
    )
    base = starts - 1
    ranks = []
    for k, piece in enumerate(pieces):
        part = so_far[k * nbuckets : (k + 1) * nbuckets, :]
        ranks.append(jnp.sum(piece.astype(jnp.float32) * (part + base), axis=0, keepdims=True))
        base = base + part[:, SORT - 1 : SORT]
    rank = jnp.concatenate(ranks, axis=1).astype(jnp.int32)

    values = whole(jnp.concatenate([places[0:1] >> 7, places[0:1] & (HALF - 1), tile[1:5, :], tile[0:2, :] * 0], axis=0))
    cells = jnp.concatenate([whole(lax.broadcasted_iota(jnp.int32, (SORT, HALF), 0))] * (slots // HALF), axis=1)
    for k in range(slots // SORT):
        local = whole(jnp.where(rank // SORT == k, rank % SORT, -1))
        chosen = jnp.maximum(1 - jnp.abs(cells - local), 0).astype(jnp.bfloat16)
        got = contract(values, chosen).astype(jnp.int32)
        at = slice(k * SORT, (k + 1) * SORT)
        out[0:1, at] = got[0:1] * HALF + got[1:2]
        out[1:5, at] = got[2:6]
    out[KNOWN : KNOWN + 1, :] = tile[KNOWN : KNOWN + 1, :]
    out[HEAD:, :] = jnp.zeros((8 - HEAD, slots), jnp.int32)
    lane = lax.broadcasted_iota(jnp.int32, (nbuckets, HALF), 1)
    firsts = jnp.sum(jnp.where(lane == ids + START, starts, 0.0), axis=0, keepdims=True).astype(jnp.int32)
    out[HEAD : HEAD + 1, :HALF] = jnp.where(lane[0:1] < START, tile[HEAD : HEAD + 1, :HALF], firsts)


def slots_of(head, half, low, high, bands):
    return head(START + half * bands + low), head(START + half * bands + high + 1)


def profiles(tile_ref, first, span, origin, nrows, ncols, size, signed_wall):
    at = pl.multiple_of(jnp.minimum(first, tile_ref.shape[-1] - size), HALF)
    tile = tile_ref[:, pl.ds(at, size)]
    slot = at + lax.broadcasted_iota(jnp.int32, (1, size), 1)
    inside = (slot >= jnp.maximum(span[0], first)) & (slot < jnp.minimum(span[1], first + size))
    signs = whole(jnp.where(inside, tile[2:5, :], 0))
    wall = wall_profiles(tile, origin[0], nrows)
    along = tent(cells_of(ncols, size), tile[1:2, :], origin[1])
    if signed_wall:
        return jnp.concatenate([wall * signs[c : c + 1, :] for c in range(3)], axis=0), along
    return wall, jnp.concatenate([along * signs[c : c + 1, :] for c in range(3)], axis=0)


def add_windows(out, sources, firsts, at_row, nrows, at_col, ncols, size, signed_wall, base, base_row):
    pairs = [profiles(s[0], f, s[1], s[2], nrows, ncols, size, signed_wall) for s, f in zip(sources, firsts)]
    wall, along = (jnp.concatenate(x, axis=1) if len(x) > 1 else x[0] for x in zip(*pairs))
    part = contract(wall, along)
    for c in range(3):
        piece = part[c * nrows : (c + 1) * nrows] if signed_wall else part[:, c * ncols : (c + 1) * ncols]
        if base is not None:
            piece = piece + base[c, pl.ds(base_row, nrows), pl.ds(at_col, ncols)]
        out[c, pl.ds(at_row, nrows), pl.ds(at_col, ncols)] = piece


def first_window(source):
    return source[1][0] // HALF * HALF


def add_first(out, sources, at_row, nrows, at_col, ncols, size, signed_wall=False, base=None, base_row=0):
    firsts = [first_window(s) for s in sources]
    add_windows(out, sources, firsts, at_row, nrows, at_col, ncols, size, signed_wall, base, base_row)


def add_rest(out, sources, at_row, nrows, at_col, ncols, size, signed_wall=False):
    for source in sources:
        first = first_window(source)

        def more(k, carry, source=source, first=first):
            start = [first + k * size]
            add_windows(out, [source], start, at_row, nrows, at_col, ncols, size, signed_wall, out, at_row)
            return carry

        lax.fori_loop(1, (source[1][1] - first + size - 1) // size, more, 0)


def reach(row, bands):
    band = row // HALF
    return jnp.maximum(band - 1, 0), jnp.minimum(band + ROWS // HALF, bands - 1)


def head_of(heads):
    return lambda lane: heads[HEAD, lane]


def own_sources(heads, tile, row, bands):
    low, high = reach(row, bands)
    return [(tile, slots_of(head_of(heads), half, low, high, bands), (row, 0)) for half in range(2)]


def side_sources(heads, tile, side, row, ncols, bands):
    low, high = reach(row, bands)
    origin = jnp.where(side == 1, -ncols, 2 * ncols)
    return [(tile, slots_of(head_of(heads), 1 - side, low, high, bands), (row, origin))]


def add_edge(out, heads, tiles, below, even_z, bands):
    cols = out.shape[2]
    row = jnp.where(below == 1, -HALF, bands * HALF)
    band = jnp.where(below == 1, 0, bands - 1)
    sources = []
    for t, half in ((0, even_z), (1, 0), (1, 1), (2, 1 - even_z)):
        column = (1 - t) * (2 * even_z - 1) * cols
        span = slots_of(lambda lane, t=t: heads[t, HEAD, lane], half, band, band, bands)
        sources.append((tiles.at[t], span, (row, column)))
    at = (0, HALF, 0, cols, EDGE_WINDOW)
    add_first(out, sources, *at, signed_wall=True, base=out)
    add_rest(out, sources, *at, signed_wall=True)


def transform(diag, shear, part):
    factors = jnp.concatenate([diag, shear, jnp.zeros((2, diag.shape[1]), jnp.float32)], axis=0).T
    a0, a1, a2 = (factors[:, k : k + 1] for k in range(3))
    b0, b1, b2 = (factors[:, 3 + k : 4 + k] for k in range(3))
    return a0 * part[0], b0 * part[0] + a1 * part[1], b1 * part[0] + b2 * part[1] + a2 * part[2]


def own_kernel(own_heads, own, out, *, bands, first):
    cols = out.shape[2]

    def add_block(block, carry):
        row = pl.multiple_of(block * ROWS, ROWS)
        sources = own_sources(own_heads, own, first + row, bands)
        add_first(out, sources, row, ROWS, 0, cols, WINDOW)
        add_rest(out, sources, row, ROWS, 0, cols, WINDOW)
        return carry

    lax.fori_loop(0, out.shape[1] // ROWS, add_block, 0)


def field_kernel(own_heads, near_heads, far_heads, own, near, far, diag, shear, *refs, bands, first):
    *raw, out, acc = refs
    cols = out.shape[2]
    ncols = cols // 2
    odd_z = own_heads[HEAD, 2] % 2
    whole_at = (0, ROWS, 0, cols, WINDOW)
    near_at = (0, ROWS, pl.multiple_of((1 - odd_z) * ncols, ncols), ncols, WINDOW)
    far_at = (0, ROWS, pl.multiple_of(odd_z * ncols, ncols), ncols, WINDOW)

    def finish(block):
        at = pl.ds(pl.multiple_of(block * ROWS, ROWS), ROWS)
        at_factors = pl.ds(pl.multiple_of(first + block * ROWS, ROWS), ROWS)
        for c, part in enumerate(transform(diag[:, at_factors], shear[:, at_factors], acc)):
            out[c, at, :] = part

    def add_block(block, carry):
        row = pl.multiple_of(first + block * ROWS, ROWS)
        from_own = own_sources(own_heads, own, row, bands)
        from_near = side_sources(near_heads, near, 1 - odd_z, row, ncols, bands)
        from_far = side_sources(far_heads, far, odd_z, row, ncols, bands)
        finish(jnp.maximum(block - 1, 0))
        base, base_row = (raw[0], pl.multiple_of(block * ROWS, ROWS)) if raw else (acc, 0)
        if not raw:
            add_first(acc, from_own, *whole_at)
        add_first(acc, from_near, *near_at, base=base, base_row=base_row)
        add_first(acc, from_far, *far_at, base=base, base_row=base_row)
        if not raw:
            add_rest(acc, from_own, *whole_at)
        add_rest(acc, from_near, *near_at)
        add_rest(acc, from_far, *far_at)
        return carry

    nblocks = out.shape[1] // ROWS
    acc[...] = jnp.zeros_like(acc)
    lax.fori_loop(0, nblocks, add_block, 0)
    finish(nblocks - 1)


def last_kernel(
    own_heads, up_heads, down_heads, near_y, far_y, over, known, upper, lower, diag, shear, mean, out, acc,
    *, bands, tiles_y, scale
):
    block = pl.program_id(0)
    rows = out.shape[1]
    nblocks = bands * HALF // rows
    at_y, odd_z = own_heads[HEAD, 1], own_heads[HEAD, 2] % 2
    odd_y = at_y % 2
    total = jnp.sum(jnp.maximum(known[...], over[...]).astype(jnp.float32), axis=1, keepdims=True)
    amplitude = jnp.sqrt(scale / total) * (1.5 / (HALF * HALF))
    for part, held in enumerate((upper, lower)):

        @pl.when(block // (nblocks // 2) == part)
        def _(held=held):
            row = pl.multiple_of((block % (nblocks // 2)) * rows, rows)
            out[...] = mean[...] + amplitude * held[:, pl.ds(row, rows), :]

    def add_beyond(heads, tiles, below):
        acc[...] = jnp.zeros_like(acc)
        add_edge(acc, heads, tiles, below, 1 - odd_z, bands)
        first = pl.multiple_of(below * (bands * HALF - HALF), HALF)
        parts = transform(diag[:, pl.ds(first, HALF)], shear[:, pl.ds(first, HALF)], acc)
        at = pl.ds(pl.multiple_of(below * (rows - HALF), HALF), HALF)
        for c, part in enumerate(parts):
            out[c, at, :] += amplitude * part

    @pl.when(block == (1 - odd_y) * (nblocks - 1))
    def _():
        add_beyond(up_heads, near_y, 1 - odd_y)

    @pl.when((block == odd_y * (nblocks - 1)) & (at_y > 0) & (at_y < tiles_y - 1))
    def _():
        add_beyond(down_heads, far_y, odd_y)


def with_known(tile, known):
    wide = jnp.pad(known, ((0, 0), (0, tile.shape[1] - known.shape[1])))
    return jnp.where(jnp.arange(tile.shape[0])[:, None] == KNOWN, wide, tile)


def packed(places, signs, count, at_y, at_z):
    slots = places.shape[-1]
    slot = jnp.arange(slots, dtype=jnp.int32)[None]
    row = jnp.arange(8, dtype=jnp.int32)[:, None]
    signs = jnp.where(slot < count, signs, 0)
    place = jnp.where(slot == 0, count, jnp.where(slot == 1, at_y, at_z))
    rest = jnp.where(row == HEAD, place, 0)
    return jnp.pad(places, ((0, 6), (0, 0))) + jnp.pad(signs, ((2, 3), (0, 0))) + rest


def body(eddy_cells, eddy_signs, eddy_counts, stress_diag, stress_shear, mean_flow):
    slots = eddy_cells.shape[-1]
    _, rows, cols = mean_flow.shape
    tiles_y, tiles_z = lax.axis_size("gy"), lax.axis_size("gz")
    at_y, at_z = lax.axis_index("gy"), lax.axis_index("gz")
    assert cols == 2 * HALF and rows % (2 * ROWS) == 0 and slots % WINDOW == 0
    bands = rows // HALF
    assert START + 2 * bands < HALF
    assert tiles_z > 2 and tiles_z & (tiles_z - 1) == 0
    assert covers(pairs_skip(tiles_y) + [pairs_near(tiles_y), pairs_over(tiles_y, 2)], tiles_y)
    bands = rows // HALF
    assert START + 2 * bands < HALF
    assert covers([pairs_near(tiles_z), pairs_far(tiles_z)] + pairs_skip(tiles_z), tiles_z)
    assert covers(pairs_skip(tiles_y) + [pairs_near(tiles_y), pairs_over(tiles_y, 2)], tiles_y)

    vmem = pl.BlockSpec(memory_space=pltpu.VMEM)
    heads = pl.BlockSpec((8, HALF), lambda i: (0, 0), memory_space=pltpu.SMEM)
    field_block = pl.BlockSpec((3, ROWS, cols), lambda i: (0, i, 0))
    field_shape = jax.ShapeDtypeStruct((3, rows, cols), jnp.float32)
    edge_heads = pl.BlockSpec((3, 8, HALF), lambda i: (0, 0, 0), memory_space=pltpu.SMEM)
    macs = 3 * rows * cols * slots

    def cost(part, moved):
        return pl.CostEstimate(flops=int(2 * macs * part), transcendentals=0, bytes_accessed=int(4 * moved * 3 * rows * cols))

    count = eddy_counts.reshape(())
    lanes = -(-tiles_y * tiles_z // HALF) * HALF
    known = jnp.where(jnp.arange(lanes, dtype=jnp.int32)[None] == at_y * tiles_z + at_z, count, 0)
    anchor = jnp.stack([at_y * rows, at_z * cols]).astype(jnp.int32)
    places = eddy_cells.reshape(2, slots) - anchor[:, None]
    own = packed(places, eddy_signs.reshape(3, slots), count, at_y, at_z)
    known, own = lax.optimization_barrier((known, own))
    for pairs in pairs_skip(tiles_y):
        known = jnp.maximum(known, lax.ppermute(known, "gy", pairs))
    own = pl.pallas_call(
        functools.partial(order_kernel, bands=bands),
        grid=(1,),
        in_specs=[heads, vmem],
        out_specs=vmem,
        out_shape=jax.ShapeDtypeStruct((8, slots), jnp.int32),
        cost_estimate=cost(0.3, 0.1),
        compiler_params=pltpu.CompilerParams(vmem_limit_bytes=24 << 20),
    )(own, own)

    own = with_known(own, known)
    near_z = lax.ppermute(own, "gz", pairs_near(tiles_z))
    far_z = lax.ppermute(own, "gz", pairs_far(tiles_z))
    others = [known, near_z[KNOWN : KNOWN + 1, :lanes], far_z[KNOWN : KNOWN + 1, :lanes]]
    for by in range(2, tiles_z):
        if tiles_z != 4 or by == 2:
            others.append(lax.ppermute(known, "gz", pairs_over(tiles_z, by)))
    known = functools.reduce(jnp.maximum, others)
    row_of_tiles = jnp.stack([far_z, own, near_z])
    one = lax.ppermute(known, "gy", pairs_near(tiles_y))
    near_y = lax.ppermute(row_of_tiles, "gy", pairs_near(tiles_y))
    far_y = lax.ppermute(row_of_tiles, "gy", pairs_inner(tiles_y))

    half = rows // 2
    half_shape = jax.ShapeDtypeStruct((3, half, cols), jnp.float32)
    params = pltpu.CompilerParams(vmem_limit_bytes=24 << 20)
    acc = pltpu.VMEM((3, ROWS, cols), jnp.float32)
    raw = pl.pallas_call(
        functools.partial(own_kernel, bands=bands, first=0),
        grid=(1,),
        in_specs=[heads, vmem],
        out_specs=vmem,
        out_shape=half_shape,
        cost_estimate=cost(0.2, 0.5),
        compiler_params=params,
    )(own, own)

    def field_part(first, *raw):
        return pl.pallas_call(
            functools.partial(field_kernel, bands=bands, first=first),
            grid=(1,),
            in_specs=[heads] * 3 + [vmem] * (5 + len(raw)),
            out_specs=vmem,
            out_shape=half_shape,
            scratch_shapes=[acc],
            cost_estimate=cost(0.2, 0.5),
            compiler_params=params,
        )(own, near_z, far_z, own, near_z, far_z, stress_diag, stress_shear, *raw)

    lower = field_part(half)
    known = jnp.maximum(known, one)
    over = lax.ppermute(known, "gy", pairs_over(tiles_y, 2))
    upper = field_part(0, raw)

    block_rows = LAST_ROWS
    last_block = pl.BlockSpec((3, block_rows, cols), lambda i: (0, i, 0))
    scale = rows * tiles_y * (cols * tiles_z) / (HALF * HALF)
    return pl.pallas_call(
        functools.partial(last_kernel, bands=bands, tiles_y=tiles_y, scale=scale),
        grid=(rows // block_rows,),
        in_specs=[heads] + [edge_heads] * 2 + [vmem] * 8 + [last_block],
        out_specs=last_block,
        out_shape=field_shape,
        scratch_shapes=[pltpu.VMEM((3, HALF, cols), jnp.float32)],
        cost_estimate=cost(0.3, 2.0),
        compiler_params=pltpu.CompilerParams(vmem_limit_bytes=24 << 20),
    )(
        own, near_y, far_y, near_y, far_y, over, known, upper, lower,
        stress_diag, stress_shear, mean_flow,
    )


def solution(mesh):
    in_specs = (
        P("gy", "gz", None, None),
        P("gy", "gz", None, None),
        P("gy", "gz"),
        P(None, "gy"),
        P(None, "gy"),
        P(None, "gy", "gz"),
    )

    return jax.shard_map(body, mesh=mesh, in_specs=in_specs, out_specs=P(None, "gy", "gz"), check_vma=False)
```

time: 56.2 us -> 42.2 us (0.75)
  the two profiles are of different devices: /device:TPU:1 before, /device:TPU:0 now
where the time goes in v2:
time: 42.2 us; the launch traced here: 42 us
  Pallas kernels  22.1 us (52%)
  starting transfers between devices  14.2 us (34%)
  waiting for transfers between devices  2.96 us (7%)
  other arithmetic  1.91 us (5%)
  between operations  0.84 us (2%)
    pallas_call x2, Pallas kernels, field_part(): pl.pallas_call(functools.partial(field_kernel, bands=bands, first=first),...  9.38 us
    pallas_call x1, Pallas kernels, body(): pl.pallas_call(functools.partial(last_kernel, bands=bands, tiles_y=tiles_...  6.77 us
    ppermute x1, starting transfers between devices, body(): near_y = lax.ppermute(row_of_tiles, 'gy', pairs_near(tiles_y))  4.34 us
    ppermute x1, starting transfers between devices, body(): known = jnp.maximum(known, lax.ppermute(known, 'gy', pairs))  4.08 us
    pallas_call x1, Pallas kernels, body(): pl.pallas_call(functools.partial(order_kernel, bands=bands), grid=(1,), i...  3.2 us
    pallas_call x1, Pallas kernels, body(): pl.pallas_call(functools.partial(own_kernel, bands=bands, first=0), grid=...  2.74 us
    ppermute x1, starting transfers between devices, body(): over = lax.ppermute(known, 'gy', pairs_over(tiles_y, 2))  2.59 us
    ppermute x1, waiting for transfers between devices, body(): one = lax.ppermute(known, 'gy', pairs_near(tiles_y))  2.49 us
  transfers between devices with their start and end apart: 8, of which 2 were waited for; matrix products, arithmetic and copies ran while one was open for 0% of the time, Pallas kernels for 36%

profile of v2, /device:TPU:0, one launch (start us, length us, event | category | flops | bytes accessed | tf_op | source)
XLA Modules:
  0.0 42.0 jit_solution(16376417382077642454)
XLA Ops:
  0.7 0.1 pad_add_fusion.1
  0.8 0.8 %bitcast_subtract_fusion = s32[2,2048]{1,0:T(2,128)S(1)} fusion(s32[1,1,2,2048]{3,2,1,0:T(2,128)} %param.6, s32[2]{0:T(128)S(1)} %pad_add_fusion.1), kind=kLoop, calls=%fused_computation.4 | loop fusion | flops 4096 | bytes 32776 | tf_op jit(solution)/shard_map/sub | solution.py:338
  1.6 0.8 %bitcast_select_fusion = s32[3,2048]{1,0:T(4,128)S(1)} fusion(s32[1,1,3,2048]{3,1,2,0:T(1,128)} %param.7, pred[2048]{0:T(1024)(128)(4,1)S(1)} %iota_compare_fusion.2), kind=kLoop, calls=%fused_computation.2 | loop fusion | flops 6144 | bytes 51200 | tf_op jit(solution)/shard_map/jit(_where)/select_n | solution.py:303
  2.3 0.1 select_add_fusion.heads.tile
  2.4 4.1 %collective-permute-start = (s32[1,128]{1,0:T(1,128)S(1)}, s32[1,128]{1,0:T(1,128)S(1)}, u32[]{:S(2)}, u32[]{:S(2)}) collective-permute-start(s32[1,128]{1,0:T(1,128)S(1)} %compare_select_fusion), channel_id=1, source_target_pairs={{0,16},{4,20},{8,24},{12,28},{16,0},{20,4},{24,8},{28,12},{1,17},{... | collective-permute-start | bytes 1544 | tf_op jit(solution)/shard_map/ppermute | solution.py:342
  6.5 3.2 %shard_map.64 = s32[8,2048]{1,0:T(8,128)S(1)} custom-call(s32[8,2048]{1,0:T(8,128)S(1)} %select_add_fusion.heads.tile, s32[8,2048]{1,0:T(8,128)S(1)} %select_add_fusion.heads.tile), custom_call_target="tpu_custom_call" | custom-call | flops 1932735232 | bytes 629145 | tf_op jit(solution)/shard_map/pallas_call | solution.py:343
  9.7 0.0 copy-start
  9.7 0.0 copy-start.1
  9.7 1.6 %collective-permute-start.5 = (s32[1,128]{1,0:T(1,128)S(1)}, s32[1,128]{1,0:T(1,128)S(1)}, u32[]{:S(2)}, u32[]{:S(2)}) collective-permute-start(s32[1,128]{1,0:T(1,128)S(1)} %max.15), channel_id=1, source_target_pairs={{0,2},{1,3},{2,0},{3,1},{4,6},{5,7},{6,4},{7,5},{8,10},{9,11},{10,... | collective-permute-start | bytes 1544 | tf_op jit(solution)/shard_map/ppermute | solution.py:359
  11.3 0.1 broadcast_select_fusion.own_heads.own
  11.4 0.1 fusion.1
  11.5 0.0 collective-permute-start.2
  11.5 0.6 %collective-permute-start.1 = (s32[8,2048]{1,0:T(8,128)S(1)}, s32[8,2048]{1,0:T(8,128)S(1)}, u32[]{:S(2)}, u32[]{:S(2)}) collective-permute-start(s32[8,2048]{1,0:T(8,128)S(1)} %broadcast_select_fusion.own_heads.own), channel_id=1, source_target_pairs={{0,3},{1,2},{2,1},{3,0},{4,7},{5,6},{6,5},{7,4},{8,11},{9,10},{10,... | collective-permute-start | bytes 196616 | tf_op jit(solution)/shard_map/ppermute | solution.py:355
  12.1 2.7 %shard_map.65.refs_0_ = f32[3,1024,256]{2,1,0:T(8,128)S(1)} custom-call(s32[8,2048]{1,0:T(8,128)S(1)} %broadcast_select_fusion.own_heads.own, s32[8,2048]{1,0:T(8,128)S(1)} %broadcast_select_fusion.own_heads.own), custom_call_target="tpu_custom_call" | custom-call | flops 1288490240 | bytes 3145728 | tf_op jit(solution)/shard_map/pallas_call | solution.py:370
  14.9 0.4 %collective-permute-done.1.far_heads.far = s32[8,2048]{1,0:T(8,128)S(1)} collective-permute-done((s32[8,2048]{1,0:T(8,128)S(1)}, s32[8,2048]{1,0:T(8,128)S(1)}, u32[]{:S(2)}, u32[]{:S(2)}) %collective-permute-start.1) | collective-permute-done | bytes 65568 | tf_op jit(solution)/shard_map/ppermute | solution.py:355
  15.3 0.9 %collective-permute-start.4 = (s32[3,8,2048]{2,1,0:T(8,128)S(1)}, s32[3,8,2048]{2,1,0:T(8,128)S(1)}, u32[]{:S(2)}, u32[]{:S(2)}) collective-permute-start(s32[3,8,2048]{2,1,0:T(8,128)S(1)} %pad_add_fusion), channel_id=1, source_target_pairs={{4,8},{8,4},{12,16},{16,12},{20,24},{24,20},{5,9},{9,5},{13,17},{1... | collective-permute-start | bytes 589832 | tf_op jit(solution)/shard_map/ppermute | solution.py:364
  16.2 4.3 %collective-permute-start.3 = (s32[3,8,2048]{2,1,0:T(8,128)S(1)}, s32[3,8,2048]{2,1,0:T(8,128)S(1)}, u32[]{:S(2)}, u32[]{:S(2)}) collective-permute-start(s32[3,8,2048]{2,1,0:T(8,128)S(1)} %pad_add_fusion), channel_id=1, source_target_pairs={{0,4},{4,0},{8,12},{12,8},{16,20},{20,16},{24,28},{28,24},{1,5},{5... | collective-permute-start | bytes 589832 | tf_op jit(solution)/shard_map/ppermute | solution.py:363
  20.6 0.0 slice-start.1
  20.6 0.1 collective-permute-start.6
  20.7 5.5 %shard_map.67.lower = f32[3,1024,256]{2,1,0:T(8,128)S(1)} custom-call(s32[8,2048]{1,0:T(8,128)S(1)} %broadcast_select_fusion.own_heads.own, s32[8,2048]{1,0:T(8,128)S(1)} %collective-permute-done.2.near_heads.near, s32[8,2048]{1,0:T(8,128)S(1)} %collective-permute-done.1.far_heads.far, s32[8,2048]{1,0:T(8,128)S(1)} %broadcast_select_fusion.own_heads.own, ...), custom_call_target="tpu_custom_call" | custom-call | flops 1288490240 | bytes 3145728 | tf_op jit(solution)/shard_map/pallas_call | solution.py:381
  26.2 2.5 %collective-permute-done.6 = s32[1,128]{1,0:T(1,128)S(1)} collective-permute-done((s32[1,128]{1,0:T(1,128)S(1)}, s32[1,128]{1,0:T(1,128)S(1)}, u32[]{:S(2)}, u32[]{:S(2)}) %collective-permute-start.6) | collective-permute-done | bytes 544 | tf_op jit(solution)/shard_map/ppermute | solution.py:362
  28.7 2.6 %collective-permute-start.7 = (s32[1,128]{1,0:T(1,128)S(1)}, s32[1,128]{1,0:T(1,128)S(1)}, u32[]{:S(2)}, u32[]{:S(2)}) collective-permute-start(s32[1,128]{1,0:T(1,128)S(1)} %max.19.known), channel_id=1, source_target_pairs={{0,8},{4,12},{8,0},{12,4},{16,24},{20,28},{24,16},{28,20},{1,9},{5... | collective-permute-start | bytes 1544 | tf_op jit(solution)/shard_map/ppermute | solution.py:394
  31.3 3.9 %shard_map.66.upper = f32[3,1024,256]{2,1,0:T(8,128)S(1)} custom-call(s32[8,2048]{1,0:T(8,128)S(1)} %broadcast_select_fusion.own_heads.own, s32[8,2048]{1,0:T(8,128)S(1)} %collective-permute-done.2.near_heads.near, s32[8,2048]{1,0:T(8,128)S(1)} %collective-permute-done.1.far_heads.far, s32[8,2048]{1,0:T(8,128)S(1)} %broadcast_select_fusion.own_heads.own, ...), custom_call_target="tpu_custom_call" | custom-call | flops 1288490240 | bytes 3145728 | tf_op jit(solution)/shard_map/pallas_call | solution.py:381
  35.2 6.8 %shard_map.68 = f32[3,2048,256]{2,1,0:T(8,128)} custom-call(s32[8,2048]{1,0:T(8,128)S(1)} %broadcast_select_fusion.own_heads.own, s32[3,8,2048]{2,1,0:T(8,128)S(1)} %collective-permute-done.3.up_heads.near_y, s32[3,8,2048]{2,1,0:T(8,128)S(1)} %collective-permute-done.4.down_heads.far_y, s32[3,8,2048]{2,1,0:T(8,128)S(1)} %collective-permute-done.3.up_heads.near_y, ...), custom_call_target="tpu_custom_call" | custom-call | flops 1932735232 | bytes 12582912 | tf_op jit(solution)/shard_map/pallas_call | solution.py:400
  (22 shorter events, 0.1 us)
Async XLA Ops:
  2.4 7.3 %collective-permute-start = (s32[1,128]{1,0:T(1,128)S(1)}, s32[1,128]{1,0:T(1,128)S(1)}, u32[]{:S(2)}, u32[]{:S(2)}) collective-permute-start(s32[1,128]{1,0:T(1,128)S(1)} %compare_select_fusion), channel_id=1, source_target_pairs={{0,16},{4,20},{8,24},{12,28},{16,0},{20,4},{24,8},{28,12},{1,17},{... | collective-permute-start | bytes 1544 | tf_op jit(solution)/shard_map/ppermute | solution.py:342
  9.7 11.0 %copy-start = (f32[3,2048]{1,0:T(4,128)S(1)}, f32[3,2048]{1,0:T(4,128)}, u32[]{:S(2)}) copy-start(f32[3,2048]{1,0:T(4,128)} %diag.5) | copy-start | bytes 73732
  9.7 11.0 %copy-start.1 = (f32[3,2048]{1,0:T(4,128)S(1)}, f32[3,2048]{1,0:T(4,128)}, u32[]{:S(2)}) copy-start(f32[3,2048]{1,0:T(4,128)} %shear.5) | copy-start | bytes 73732
  9.7 10.8 %collective-permute-start.5 = (s32[1,128]{1,0:T(1,128)S(1)}, s32[1,128]{1,0:T(1,128)S(1)}, u32[]{:S(2)}, u32[]{:S(2)}) collective-permute-start(s32[1,128]{1,0:T(1,128)S(1)} %max.15), channel_id=1, source_target_pairs={{0,2},{1,3},{2,0},{3,1},{4,6},{5,7},{6,4},{7,5},{8,10},{9,11},{10,... | collective-permute-start | bytes 1544 | tf_op jit(solution)/shard_map/ppermute | solution.py:359
  11.5 3.4 %collective-permute-start.2 = (s32[8,2048]{1,0:T(8,128)S(1)}, s32[8,2048]{1,0:T(8,128)S(1)}, u32[]{:S(2)}, u32[]{:S(2)}) collective-permute-start(s32[8,2048]{1,0:T(8,128)S(1)} %broadcast_select_fusion.own_heads.own), channel_id=1, source_target_pairs={{0,1},{1,0},{2,3},{3,2},{4,5},{5,4},{6,7},{7,6},{8,9},{9,8},{10,11... | collective-permute-start | bytes 196616 | tf_op jit(solution)/shard_map/ppermute | solution.py:354
  11.5 3.8 %collective-permute-start.1 = (s32[8,2048]{1,0:T(8,128)S(1)}, s32[8,2048]{1,0:T(8,128)S(1)}, u32[]{:S(2)}, u32[]{:S(2)}) collective-permute-start(s32[8,2048]{1,0:T(8,128)S(1)} %broadcast_select_fusion.own_heads.own), channel_id=1, source_target_pairs={{0,3},{1,2},{2,1},{3,0},{4,7},{5,6},{6,5},{7,4},{8,11},{9,10},{10,... | collective-permute-start | bytes 196616 | tf_op jit(solution)/shard_map/ppermute | solution.py:355
  12.1 23.1 %slice-start = ((s8[6291456]{0:T(1024)(128)(4,1)}), s8[4194304]{0:T(1024)(128)(4,1)S(1)}, s32[]{:S(2)}) async-start(s8[6291456]{0:T(1024)(128)(4,1)} %bitcast.15), calls=%async_computation | async-start | bytes 8388608
  15.3 19.8 %collective-permute-start.4 = (s32[3,8,2048]{2,1,0:T(8,128)S(1)}, s32[3,8,2048]{2,1,0:T(8,128)S(1)}, u32[]{:S(2)}, u32[]{:S(2)}) collective-permute-start(s32[3,8,2048]{2,1,0:T(8,128)S(1)} %pad_add_fusion), channel_id=1, source_target_pairs={{4,8},{8,4},{12,16},{16,12},{20,24},{24,20},{5,9},{9,5},{13,17},{1... | collective-permute-start | bytes 589832 | tf_op jit(solution)/shard_map/ppermute | solution.py:364
  16.2 19.0 %collective-permute-start.3 = (s32[3,8,2048]{2,1,0:T(8,128)S(1)}, s32[3,8,2048]{2,1,0:T(8,128)S(1)}, u32[]{:S(2)}, u32[]{:S(2)}) collective-permute-start(s32[3,8,2048]{2,1,0:T(8,128)S(1)} %pad_add_fusion), channel_id=1, source_target_pairs={{0,4},{4,0},{8,12},{12,8},{16,20},{20,16},{24,28},{28,24},{1,5},{5... | collective-permute-start | bytes 589832 | tf_op jit(solution)/shard_map/ppermute | solution.py:363
  20.6 14.6 %slice-start.1 = ((s8[6291456]{0:T(1024)(128)(4,1)}), s8[2097152]{0:T(1024)(128)(4,1)S(1)}, s32[]{:S(2)}) async-start(s8[6291456]{0:T(1024)(128)(4,1)} %bitcast.15), calls=%async_computation.1 | async-start | bytes 4194304
  20.6 8.1 %collective-permute-start.6 = (s32[1,128]{1,0:T(1,128)S(1)}, s32[1,128]{1,0:T(1,128)S(1)}, u32[]{:S(2)}, u32[]{:S(2)}) collective-permute-start(s32[1,128]{1,0:T(1,128)S(1)} %fusion), channel_id=1, source_target_pairs={{0,4},{4,0},{8,12},{12,8},{16,20},{20,16},{24,28},{28,24},{1,5},{5... | collective-permute-start | bytes 1544 | tf_op jit(solution)/shard_map/ppermute | solution.py:362
  28.7 6.5 %collective-permute-start.7 = (s32[1,128]{1,0:T(1,128)S(1)}, s32[1,128]{1,0:T(1,128)S(1)}, u32[]{:S(2)}, u32[]{:S(2)}) collective-permute-start(s32[1,128]{1,0:T(1,128)S(1)} %max.19.known), channel_id=1, source_target_pairs={{0,8},{4,12},{8,0},{12,4},{16,24},{20,28},{24,16},{28,20},{1,9},{5... | collective-permute-start | bytes 1544 | tf_op jit(solution)/shard_map/ppermute | solution.py:394

commit v3 on v2

--- a/solution.py
+++ b/solution.py
@@ -10,7 +10,7 @@
 
 HALF = 128
 ROWS = 512
-LAST_ROWS = 256
+LAST_ROWS = 1024
 WINDOW = 512
 EDGE_WINDOW = 256
 SORT = 256
@@ -72,12 +72,13 @@
     return lax.dot_general(a, b, (((1,), (1,)), ((), ())), preferred_element_type=jnp.float32)
 
 
-def order_kernel(heads, tile, out, *, bands):
-    slots = tile.shape[1]
+def order_kernel(count, cells, signs, out, *, bands, cols):
+    slots = cells.shape[1]
+    at_y, at_z = lax.axis_index("gy"), lax.axis_index("gz")
     nbuckets = -(-(2 * bands + 1) // 16) * 16
-    places = tile[0:2, :]
+    places = jnp.concatenate([cells[0:1, :] - at_y * (bands * HALF), cells[1:2, :] - at_z * cols], axis=0)
     slot = lax.broadcasted_iota(jnp.int32, (1, slots), 1)
-    bucket = jnp.where(slot < heads[HEAD, 0], (places[1:2] >> 7) * bands + (places[0:1] >> 7), 2 * bands)
+    bucket = jnp.where(slot < count[0, 0], (places[1:2] >> 7) * bands + (places[0:1] >> 7), 2 * bands)
     ids = lax.broadcasted_iota(jnp.int32, (nbuckets, HALF), 0)
     wide_ids = jnp.concatenate([ids] * (slots // HALF), axis=1)
     starts = jnp.sum((bucket < wide_ids).astype(jnp.float32), axis=1, keepdims=True)
@@ -98,7 +99,9 @@
         base = base + part[:, SORT - 1 : SORT]
     rank = jnp.concatenate(ranks, axis=1).astype(jnp.int32)
 
-    values = whole(jnp.concatenate([places[0:1] >> 7, places[0:1] & (HALF - 1), tile[1:5, :], tile[0:2, :] * 0], axis=0))
+    live = jnp.where(slot < count[0, 0], signs[...], 0)
+    parts = [places[0:1] >> 7, places[0:1] & (HALF - 1), places[1:2], live, jnp.zeros((2, slots), jnp.int32)]
+    values = whole(jnp.concatenate(parts, axis=0))
     cells = jnp.concatenate([whole(lax.broadcasted_iota(jnp.int32, (SORT, HALF), 0))] * (slots // HALF), axis=1)
     for k in range(slots // SORT):
         local = whole(jnp.where(rank // SORT == k, rank % SORT, -1))
@@ -107,11 +110,11 @@
         at = slice(k * SORT, (k + 1) * SORT)
         out[0:1, at] = got[0:1] * HALF + got[1:2]
         out[1:5, at] = got[2:6]
-    out[KNOWN : KNOWN + 1, :] = tile[KNOWN : KNOWN + 1, :]
-    out[HEAD:, :] = jnp.zeros((8 - HEAD, slots), jnp.int32)
+    out[KNOWN:, :] = jnp.zeros((8 - KNOWN, slots), jnp.int32)
     lane = lax.broadcasted_iota(jnp.int32, (nbuckets, HALF), 1)
     firsts = jnp.sum(jnp.where(lane == ids + START, starts, 0.0), axis=0, keepdims=True).astype(jnp.int32)
-    out[HEAD : HEAD + 1, :HALF] = jnp.where(lane[0:1] < START, tile[HEAD : HEAD + 1, :HALF], firsts)
+    place = jnp.where(lane[0:1] == 0, count[0, 0], jnp.where(lane[0:1] == 1, at_y, at_z))
+    out[HEAD : HEAD + 1, :HALF] = jnp.where(lane[0:1] < START, place, firsts)
 
 
 def slots_of(head, half, low, high, bands):
@@ -177,10 +180,11 @@
     return [(tile, slots_of(head_of(heads), half, low, high, bands), (row, 0)) for half in range(2)]
 
 
-def side_sources(heads, tile, side, row, ncols, bands):
+def side_sources(heads, tiles, place, side, row, ncols, bands):
     low, high = reach(row, bands)
-    origin = jnp.where(side == 1, -ncols, 2 * ncols)
-    return [(tile, slots_of(head_of(heads), 1 - side, low, high, bands), (row, origin))]
+    origin = -ncols if side else 2 * ncols
+    span = slots_of(lambda lane: heads[place, HEAD, lane], 1 - side, low, high, bands)
+    return [(tiles.at[place], span, (row, origin))]
 
 
 def add_edge(out, heads, tiles, below, even_z, bands):
@@ -217,46 +221,44 @@
     lax.fori_loop(0, out.shape[1] // ROWS, add_block, 0)
 
 
-def field_kernel(own_heads, near_heads, far_heads, own, near, far, diag, shear, *refs, bands, first):
-    *raw, out, acc = refs
+def field_kernel(own_heads, heads, own, tiles, diag, shear, raw, out, acc, *, bands):
     cols = out.shape[2]
     ncols = cols // 2
     odd_z = own_heads[HEAD, 2] % 2
     whole_at = (0, ROWS, 0, cols, WINDOW)
-    near_at = (0, ROWS, pl.multiple_of((1 - odd_z) * ncols, ncols), ncols, WINDOW)
-    far_at = (0, ROWS, pl.multiple_of(odd_z * ncols, ncols), ncols, WINDOW)
+    left_at = (0, ROWS, 0, ncols, WINDOW)
+    right_at = (0, ROWS, ncols, ncols, WINDOW)
 
     def finish(block):
         at = pl.ds(pl.multiple_of(block * ROWS, ROWS), ROWS)
-        at_factors = pl.ds(pl.multiple_of(first + block * ROWS, ROWS), ROWS)
-        for c, part in enumerate(transform(diag[:, at_factors], shear[:, at_factors], acc)):
+        for c, part in enumerate(transform(diag[:, at], shear[:, at], acc)):
             out[c, at, :] = part
 
-    def add_block(block, carry):
-        row = pl.multiple_of(first + block * ROWS, ROWS)
+    def add_block(block, with_own):
+        row = pl.multiple_of(block * ROWS, ROWS)
         from_own = own_sources(own_heads, own, row, bands)
-        from_near = side_sources(near_heads, near, 1 - odd_z, row, ncols, bands)
-        from_far = side_sources(far_heads, far, odd_z, row, ncols, bands)
+        from_left = side_sources(heads, tiles, 2 * odd_z, 0, row, ncols, bands)
+        from_right = side_sources(heads, tiles, 2 - 2 * odd_z, 1, row, ncols, bands)
         finish(jnp.maximum(block - 1, 0))
-        base, base_row = (raw[0], pl.multiple_of(block * ROWS, ROWS)) if raw else (acc, 0)
-        if not raw:
+        base, base_row = (acc, 0) if with_own else (raw, row)
+        if with_own:
             add_first(acc, from_own, *whole_at)
-        add_first(acc, from_near, *near_at, base=base, base_row=base_row)
-        add_first(acc, from_far, *far_at, base=base, base_row=base_row)
-        if not raw:
+        add_first(acc, from_left, *left_at, base=base, base_row=base_row)
+        add_first(acc, from_right, *right_at, base=base, base_row=base_row)
+        if with_own:
             add_rest(acc, from_own, *whole_at)
-        add_rest(acc, from_near, *near_at)
-        add_rest(acc, from_far, *far_at)
-        return carry
-
-    nblocks = out.shape[1] // ROWS
+        add_rest(acc, from_left, *left_at)
+        add_rest(acc, from_right, *right_at)
+
+    nblocks, ready = out.shape[1] // ROWS, raw.shape[1] // ROWS
     acc[...] = jnp.zeros_like(acc)
-    lax.fori_loop(0, nblocks, add_block, 0)
+    lax.fori_loop(0, ready, lambda k, x: (add_block(k, False), x)[1], 0)
+    lax.fori_loop(ready, nblocks, lambda k, x: (add_block(k, True), x)[1], 0)
     finish(nblocks - 1)
 
 
 def last_kernel(
-    own_heads, up_heads, down_heads, near_y, far_y, over, known, upper, lower, diag, shear, mean, out, acc,
+    own_heads, up_heads, down_heads, near_y, far_y, over, known, field, diag, shear, mean, out, acc,
     *, bands, tiles_y, scale
 ):
     block = pl.program_id(0)
@@ -266,12 +268,8 @@
     odd_y = at_y % 2
     total = jnp.sum(jnp.maximum(known[...], over[...]).astype(jnp.float32), axis=1, keepdims=True)
     amplitude = jnp.sqrt(scale / total) * (1.5 / (HALF * HALF))
-    for part, held in enumerate((upper, lower)):
-
-        @pl.when(block // (nblocks // 2) == part)
-        def _(held=held):
-            row = pl.multiple_of((block % (nblocks // 2)) * rows, rows)
-            out[...] = mean[...] + amplitude * held[:, pl.ds(row, rows), :]
+    at_block = pl.ds(pl.multiple_of(block * rows, rows), rows)
+    out[...] = mean[:, at_block, :] + amplitude * field[:, at_block, :]
 
     def add_beyond(heads, tiles, below):
         acc[...] = jnp.zeros_like(acc)
@@ -294,16 +292,6 @@
 def with_known(tile, known):
     wide = jnp.pad(known, ((0, 0), (0, tile.shape[1] - known.shape[1])))
     return jnp.where(jnp.arange(tile.shape[0])[:, None] == KNOWN, wide, tile)
-
-
-def packed(places, signs, count, at_y, at_z):
-    slots = places.shape[-1]
-    slot = jnp.arange(slots, dtype=jnp.int32)[None]
-    row = jnp.arange(8, dtype=jnp.int32)[:, None]
-    signs = jnp.where(slot < count, signs, 0)
-    place = jnp.where(slot == 0, count, jnp.where(slot == 1, at_y, at_z))
-    rest = jnp.where(row == HEAD, place, 0)
-    return jnp.pad(places, ((0, 6), (0, 0))) + jnp.pad(signs, ((2, 3), (0, 0))) + rest
 
 
 def body(eddy_cells, eddy_signs, eddy_counts, stress_diag, stress_shear, mean_flow):
@@ -334,21 +322,17 @@
     count = eddy_counts.reshape(())
     lanes = -(-tiles_y * tiles_z // HALF) * HALF
     known = jnp.where(jnp.arange(lanes, dtype=jnp.int32)[None] == at_y * tiles_z + at_z, count, 0)
-    anchor = jnp.stack([at_y * rows, at_z * cols]).astype(jnp.int32)
-    places = eddy_cells.reshape(2, slots) - anchor[:, None]
-    own = packed(places, eddy_signs.reshape(3, slots), count, at_y, at_z)
-    known, own = lax.optimization_barrier((known, own))
     for pairs in pairs_skip(tiles_y):
         known = jnp.maximum(known, lax.ppermute(known, "gy", pairs))
     own = pl.pallas_call(
-        functools.partial(order_kernel, bands=bands),
+        functools.partial(order_kernel, bands=bands, cols=cols),
         grid=(1,),
-        in_specs=[heads, vmem],
+        in_specs=[pl.BlockSpec(memory_space=pltpu.SMEM), vmem, vmem],
         out_specs=vmem,
         out_shape=jax.ShapeDtypeStruct((8, slots), jnp.int32),
         cost_estimate=cost(0.3, 0.1),
         compiler_params=pltpu.CompilerParams(vmem_limit_bytes=24 << 20),
-    )(own, own)
+    )(eddy_counts, eddy_cells.reshape(2, slots), eddy_signs.reshape(3, slots))
 
     own = with_known(own, known)
     near_z = lax.ppermute(own, "gz", pairs_near(tiles_z))
@@ -377,22 +361,18 @@
         compiler_params=params,
     )(own, own)
 
-    def field_part(first, *raw):
-        return pl.pallas_call(
-            functools.partial(field_kernel, bands=bands, first=first),
-            grid=(1,),
-            in_specs=[heads] * 3 + [vmem] * (5 + len(raw)),
-            out_specs=vmem,
-            out_shape=half_shape,
-            scratch_shapes=[acc],
-            cost_estimate=cost(0.2, 0.5),
-            compiler_params=params,
-        )(own, near_z, far_z, own, near_z, far_z, stress_diag, stress_shear, *raw)
-
-    lower = field_part(half)
     known = jnp.maximum(known, one)
     over = lax.ppermute(known, "gy", pairs_over(tiles_y, 2))
-    upper = field_part(0, raw)
+    field = pl.pallas_call(
+        functools.partial(field_kernel, bands=bands),
+        grid=(1,),
+        in_specs=[heads, edge_heads] + [vmem] * 5,
+        out_specs=vmem,
+        out_shape=field_shape,
+        scratch_shapes=[acc],
+        cost_estimate=cost(0.4, 1.0),
+        compiler_params=params,
+    )(own, row_of_tiles, own, row_of_tiles, stress_diag, stress_shear, raw)
 
     block_rows = LAST_ROWS
     last_block = pl.BlockSpec((3, block_rows, cols), lambda i: (0, i, 0))
@@ -400,14 +380,14 @@
     return pl.pallas_call(
         functools.partial(last_kernel, bands=bands, tiles_y=tiles_y, scale=scale),
         grid=(rows // block_rows,),
-        in_specs=[heads] + [edge_heads] * 2 + [vmem] * 8 + [last_block],
+        in_specs=[heads] + [edge_heads] * 2 + [vmem] * 8,
         out_specs=last_block,
         out_shape=field_shape,
         scratch_shapes=[pltpu.VMEM((3, HALF, cols), jnp.float32)],
         cost_estimate=cost(0.3, 2.0),
         compiler_params=pltpu.CompilerParams(vmem_limit_bytes=24 << 20),
     )(
-        own, near_y, far_y, near_y, far_y, over, known, upper, lower,
+        own, near_y, far_y, near_y, far_y, over, known, field,
         stress_diag, stress_shear, mean_flow,
     )
 

time: 42.2 us -> 34 us (0.81)
  Pallas kernels: 22.1 us -> 17.3 us
  waiting for transfers between devices: 2.96 us -> 0.45 us
  other arithmetic: 1.91 us -> 0.19 us
  local copies, waits for them, and re-layouts: 0.03 us -> 1.48 us
  starting transfers between devices: 14.2 us -> 13.2 us
    pallas_call x3 -> x2, Pallas kernels: 12.6 us -> 9.59 us  [the longest x1 6.98 us: body(): pl.pallas_call(functools.partial(field_kernel, bands=bands), grid=(1,), i...]
    ppermute x1, starting transfers between devices: 2.59 us -> 0.07 us  [body(): over = lax.ppermute(known, 'gy', pairs_over(tiles_y, 2))]
    ppermute x1, waiting for transfers between devices: 2.49 us -> 0.01 us  [body(): one = lax.ppermute(known, 'gy', pairs_near(tiles_y))]
    pallas_call x1, Pallas kernels: 6.77 us -> 4.93 us  [body(): pl.pallas_call(functools.partial(last_kernel, bands=bands, tiles_y=tiles_...]
    ppermute x1, starting transfers between devices: 0.09 us -> 1.58 us  [body(): one = lax.ppermute(known, 'gy', pairs_near(tiles_y))]
    unnamed x8 -> x11, local copies, waits for them, and re-layouts: 0.02 us -> 1.48 us
    sub x1 -> x0, other arithmetic: 0.79 us -> none  [body(): places = eddy_cells.reshape(2, slots) - anchor[:, None]]
    select_n x2 -> x0, other arithmetic: 0.76 us -> none  [the longest x1 0.76 us: packed(): signs = jnp.where(slot < count, signs, 0)]
  transfers between devices with their start and end apart: 8 -> 8, of which waited for: 2 -> 1; matrix products, arithmetic and copies ran while one was open for 0% -> 3% of each run, Pallas kernels for 36% -> 37%
where the time goes in v3:
time: 34 us; the launch traced here: 33.4 us
  Pallas kernels  17.3 us (51%)
  starting transfers between devices  13.2 us (39%)
  local copies, waits for them, and re-layouts  1.48 us (4%)
  between operations  0.84 us (2%)
  waiting for transfers between devices  0.45 us (1%)
    pallas_call x1, Pallas kernels, body(): pl.pallas_call(functools.partial(field_kernel, bands=bands), grid=(1,), i...  6.98 us
    pallas_call x1, Pallas kernels, body(): pl.pallas_call(functools.partial(last_kernel, bands=bands, tiles_y=tiles_...  4.93 us
    ppermute x1, starting transfers between devices, body(): near_y = lax.ppermute(row_of_tiles, 'gy', pairs_near(tiles_y))  4.34 us
    ppermute x1, starting transfers between devices, body(): known = jnp.maximum(known, lax.ppermute(known, 'gy', pairs))  4.13 us
    pallas_call x1, Pallas kernels, body(): pl.pallas_call(functools.partial(own_kernel, bands=bands, first=0), grid=...  2.74 us
    pallas_call x1, Pallas kernels, body(): pl.pallas_call(functools.partial(order_kernel, bands=bands, cols=cols), g...  2.61 us
    ppermute x1, starting transfers between devices, body(): one = lax.ppermute(known, 'gy', pairs_near(tiles_y))  1.58 us
    ppermute x1, starting transfers between devices, body(): others.append(lax.ppermute(known, 'gz', pairs_over(tiles_z, by)))  1.56 us
  transfers between devices with their start and end apart: 8, of which 1 were waited for; matrix products, arithmetic and copies ran while one was open for 3% of the time, Pallas kernels for 37%

profile of v3, /device:TPU:0, one launch (start us, length us, event | category | flops | bytes accessed | tf_op | source)
XLA Modules:
  0.0 33.4 jit_solution(9995627109359694502)
XLA Ops:
  0.7 4.1 %collective-permute-start = (s32[1,128]{1,0:T(1,128)S(1)}, s32[1,128]{1,0:T(1,128)S(1)}, u32[]{:S(2)}, u32[]{:S(2)}) collective-permute-start(s32[1,128]{1,0:T(1,128)S(1)} %compare_select_fusion), channel_id=1, source_target_pairs={{0,16},{4,20},{8,24},{12,28},{16,0},{20,4},{24,8},{28,12},{1,17},{... | collective-permute-start | bytes 1544 | tf_op jit(solution)/shard_map/ppermute | solution.py:326
  4.8 0.8 %copy.9 = s32[1,1,3,2048]{3,2,1,0:T(4,128)S(1)} copy(s32[1,1,3,2048]{3,1,2,0:T(1,128)} %param.7) | data formatting | bytes 49152
  5.5 0.0 copy-start.2
  5.6 0.7 %copy-done.2 = s32[1,1,2,2048]{3,2,1,0:T(2,128)S(1)} copy-done((s32[1,1,2,2048]{3,2,1,0:T(2,128)S(1)}, s32[1,1,2,2048]{3,2,1,0:T(2,128)}, u32[]{:S(2)}) %copy-start.2) | copy-done | bytes 16408
  6.3 2.6 %shard_map.64 = s32[8,2048]{1,0:T(8,128)S(1)} custom-call(s32[1,1]{1,0:T(1,128)} %copy.10.count, s32[2,2048]{1,0:T(2,128)S(1)} %bitcast.15, s32[3,2048]{1,0:T(4,128)S(1)} %bitcast.14), custom_call_target="tpu_custom_call" | custom-call | flops 1932735232 | bytes 629145 | tf_op jit(solution)/shard_map/pallas_call | solution.py:327
  8.9 0.0 collective-permute-done
  8.9 1.6 %collective-permute-start.5 = (s32[1,128]{1,0:T(1,128)S(1)}, s32[1,128]{1,0:T(1,128)S(1)}, u32[]{:S(2)}, u32[]{:S(2)}) collective-permute-start(s32[1,128]{1,0:T(1,128)S(1)} %fusion.2), channel_id=1, source_target_pairs={{0,2},{1,3},{2,0},{3,1},{4,6},{5,7},{6,4},{7,5},{8,10},{9,11},{10,... | collective-permute-start | bytes 1544 | tf_op jit(solution)/shard_map/ppermute | solution.py:343
  10.5 0.1 broadcast_select_fusion.own_heads.own
  10.6 0.1 fusion.1
  10.6 0.0 collective-permute-start.2
  10.7 0.6 %collective-permute-start.1 = (s32[8,2048]{1,0:T(8,128)S(1)}, s32[8,2048]{1,0:T(8,128)S(1)}, u32[]{:S(2)}, u32[]{:S(2)}) collective-permute-start(s32[8,2048]{1,0:T(8,128)S(1)} %broadcast_select_fusion.own_heads.own), channel_id=1, source_target_pairs={{0,3},{1,2},{2,1},{3,0},{4,7},{5,6},{6,5},{7,4},{8,11},{9,10},{10,... | collective-permute-start | bytes 196616 | tf_op jit(solution)/shard_map/ppermute | solution.py:339
  11.3 2.7 %shard_map.65.raw = f32[3,1024,256]{2,1,0:T(8,128)S(1)} custom-call(s32[8,2048]{1,0:T(8,128)S(1)} %broadcast_select_fusion.own_heads.own, s32[8,2048]{1,0:T(8,128)S(1)} %broadcast_select_fusion.own_heads.own), custom_call_target="tpu_custom_call" | custom-call | flops 1288490240 | bytes 3145728 | tf_op jit(solution)/shard_map/pallas_call | solution.py:354
  14.1 0.0 collective-permute-done.5
  14.1 0.0 collective-permute-done.2
  14.1 0.4 %collective-permute-done.1 = s32[8,2048]{1,0:T(8,128)S(1)} collective-permute-done((s32[8,2048]{1,0:T(8,128)S(1)}, s32[8,2048]{1,0:T(8,128)S(1)}, u32[]{:S(2)}, u32[]{:S(2)}) %collective-permute-start.1) | collective-permute-done | bytes 65568 | tf_op jit(solution)/shard_map/ppermute | solution.py:339
  14.5 1.6 %collective-permute-start.6 = (s32[1,128]{1,0:T(1,128)S(1)}, s32[1,128]{1,0:T(1,128)S(1)}, u32[]{:S(2)}, u32[]{:S(2)}) collective-permute-start(s32[1,128]{1,0:T(1,128)S(1)} %fusion), channel_id=1, source_target_pairs={{0,4},{4,0},{8,12},{12,8},{16,20},{20,16},{24,28},{28,24},{1,5},{5... | collective-permute-start | bytes 1544 | tf_op jit(solution)/shard_map/ppermute | solution.py:346
  16.1 0.9 %collective-permute-start.4 = (s32[3,8,2048]{2,1,0:T(8,128)S(1)}, s32[3,8,2048]{2,1,0:T(8,128)S(1)}, u32[]{:S(2)}, u32[]{:S(2)}) collective-permute-start(s32[3,8,2048]{2,1,0:T(8,128)S(1)} %pad_add_fusion.heads.tiles), channel_id=1, source_target_pairs={{4,8},{8,4},{12,16},{16,12},{20,24},{24,20},{5,9},{9,5},{13,17},{1... | collective-permute-start | bytes 589832 | tf_op jit(solution)/shard_map/ppermute | solution.py:348
  17.0 4.3 %collective-permute-start.3 = (s32[3,8,2048]{2,1,0:T(8,128)S(1)}, s32[3,8,2048]{2,1,0:T(8,128)S(1)}, u32[]{:S(2)}, u32[]{:S(2)}) collective-permute-start(s32[3,8,2048]{2,1,0:T(8,128)S(1)} %pad_add_fusion.heads.tiles), channel_id=1, source_target_pairs={{0,4},{4,0},{8,12},{12,8},{16,20},{20,16},{24,28},{28,24},{1,5},{5... | collective-permute-start | bytes 589832 | tf_op jit(solution)/shard_map/ppermute | solution.py:347
  21.3 0.0 collective-permute-done.6
  21.3 0.1 collective-permute-start.7
  21.4 7.0 %shard_map.66.field = f32[3,2048,256]{2,1,0:T(8,128)S(1)} custom-call(s32[8,2048]{1,0:T(8,128)S(1)} %broadcast_select_fusion.own_heads.own, s32[3,8,2048]{2,1,0:T(8,128)S(1)} %pad_add_fusion.heads.tiles, s32[8,2048]{1,0:T(8,128)S(1)} %broadcast_select_fusion.own_heads.own, s32[3,8,2048]{2,1,0:T(8,128)S(1)} %pad_add_fusion.heads.tiles, ...), custom_call_target="tpu_custom_call" | custom-call | flops 2576980480 | bytes 6291456 | tf_op jit(solution)/shard_map/pallas_call | solution.py:366
  28.4 0.0 collective-permute-done.4.down_heads.far_y
  28.4 0.0 collective-permute-done.3.up_heads.near_y
  28.5 4.9 %shard_map.67 = f32[3,2048,256]{2,1,0:T(8,128)} custom-call(s32[8,2048]{1,0:T(8,128)S(1)} %broadcast_select_fusion.own_heads.own, s32[3,8,2048]{2,1,0:T(8,128)S(1)} %collective-permute-done.3.up_heads.near_y, s32[3,8,2048]{2,1,0:T(8,128)S(1)} %collective-permute-done.4.down_heads.far_y, s32[3,8,2048]{2,1,0:T(8,128)S(1)} %collective-permute-done.3.up_heads.near_y, ...), custom_call_target="tpu_custom_call" | custom-call | flops 1932735232 | bytes 12582912 | tf_op jit(solution)/shard_map/pallas_call | solution.py:380
  (17 shorter events, 0.1 us)
Async XLA Ops:
  0.7 8.2 %collective-permute-start = (s32[1,128]{1,0:T(1,128)S(1)}, s32[1,128]{1,0:T(1,128)S(1)}, u32[]{:S(2)}, u32[]{:S(2)}) collective-permute-start(s32[1,128]{1,0:T(1,128)S(1)} %compare_select_fusion), channel_id=1, source_target_pairs={{0,16},{4,20},{8,24},{12,28},{16,0},{20,4},{24,8},{28,12},{1,17},{... | collective-permute-start | bytes 1544 | tf_op jit(solution)/shard_map/ppermute | solution.py:326
  5.5 0.7 %copy-start.2 = (s32[1,1,2,2048]{3,2,1,0:T(2,128)S(1)}, s32[1,1,2,2048]{3,2,1,0:T(2,128)}, u32[]{:S(2)}) copy-start(s32[1,1,2,2048]{3,2,1,0:T(2,128)} %param.6) | copy-start | bytes 49156
  6.3 15.1 %copy-start = (f32[3,2048]{1,0:T(4,128)S(1)}, f32[3,2048]{1,0:T(4,128)}, u32[]{:S(2)}) copy-start(f32[3,2048]{1,0:T(4,128)} %diag.3) | copy-start | bytes 73732
  6.3 15.1 %copy-start.1 = (f32[3,2048]{1,0:T(4,128)S(1)}, f32[3,2048]{1,0:T(4,128)}, u32[]{:S(2)}) copy-start(f32[3,2048]{1,0:T(4,128)} %shear.3) | copy-start | bytes 73732
  8.9 5.1 %collective-permute-start.5 = (s32[1,128]{1,0:T(1,128)S(1)}, s32[1,128]{1,0:T(1,128)S(1)}, u32[]{:S(2)}, u32[]{:S(2)}) collective-permute-start(s32[1,128]{1,0:T(1,128)S(1)} %fusion.2), channel_id=1, source_target_pairs={{0,2},{1,3},{2,0},{3,1},{4,6},{5,7},{6,4},{7,5},{8,10},{9,11},{10,... | collective-permute-start | bytes 1544 | tf_op jit(solution)/shard_map/ppermute | solution.py:343
  10.6 3.4 %collective-permute-start.2 = (s32[8,2048]{1,0:T(8,128)S(1)}, s32[8,2048]{1,0:T(8,128)S(1)}, u32[]{:S(2)}, u32[]{:S(2)}) collective-permute-start(s32[8,2048]{1,0:T(8,128)S(1)} %broadcast_select_fusion.own_heads.own), channel_id=1, source_target_pairs={{0,1},{1,0},{2,3},{3,2},{4,5},{5,4},{6,7},{7,6},{8,9},{9,8},{10,11... | collective-permute-start | bytes 196616 | tf_op jit(solution)/shard_map/ppermute | solution.py:338
  10.7 3.8 %collective-permute-start.1 = (s32[8,2048]{1,0:T(8,128)S(1)}, s32[8,2048]{1,0:T(8,128)S(1)}, u32[]{:S(2)}, u32[]{:S(2)}) collective-permute-start(s32[8,2048]{1,0:T(8,128)S(1)} %broadcast_select_fusion.own_heads.own), channel_id=1, source_target_pairs={{0,3},{1,2},{2,1},{3,0},{4,7},{5,6},{6,5},{7,4},{8,11},{9,10},{10,... | collective-permute-start | bytes 196616 | tf_op jit(solution)/shard_map/ppermute | solution.py:339
  11.3 17.1 %slice-start = ((s8[6291456]{0:T(1024)(128)(4,1)}), s8[4194304]{0:T(1024)(128)(4,1)S(1)}, s32[]{:S(2)}) async-start(s8[6291456]{0:T(1024)(128)(4,1)} %bitcast.12), calls=%async_computation | async-start | bytes 8388608
  14.5 6.8 %collective-permute-start.6 = (s32[1,128]{1,0:T(1,128)S(1)}, s32[1,128]{1,0:T(1,128)S(1)}, u32[]{:S(2)}, u32[]{:S(2)}) collective-permute-start(s32[1,128]{1,0:T(1,128)S(1)} %fusion), channel_id=1, source_target_pairs={{0,4},{4,0},{8,12},{12,8},{16,20},{20,16},{24,28},{28,24},{1,5},{5... | collective-permute-start | bytes 1544 | tf_op jit(solution)/shard_map/ppermute | solution.py:346
  16.1 12.3 %collective-permute-start.4 = (s32[3,8,2048]{2,1,0:T(8,128)S(1)}, s32[3,8,2048]{2,1,0:T(8,128)S(1)}, u32[]{:S(2)}, u32[]{:S(2)}) collective-permute-start(s32[3,8,2048]{2,1,0:T(8,128)S(1)} %pad_add_fusion.heads.tiles), channel_id=1, source_target_pairs={{4,8},{8,4},{12,16},{16,12},{20,24},{24,20},{5,9},{9,5},{13,17},{1... | collective-permute-start | bytes 589832 | tf_op jit(solution)/shard_map/ppermute | solution.py:348
  17.0 11.5 %collective-permute-start.3 = (s32[3,8,2048]{2,1,0:T(8,128)S(1)}, s32[3,8,2048]{2,1,0:T(8,128)S(1)}, u32[]{:S(2)}, u32[]{:S(2)}) collective-permute-start(s32[3,8,2048]{2,1,0:T(8,128)S(1)} %pad_add_fusion.heads.tiles), channel_id=1, source_target_pairs={{0,4},{4,0},{8,12},{12,8},{16,20},{20,16},{24,28},{28,24},{1,5},{5... | collective-permute-start | bytes 589832 | tf_op jit(solution)/shard_map/ppermute | solution.py:347
  21.3 7.1 %slice-start.1 = ((s8[6291456]{0:T(1024)(128)(4,1)}), s8[2097152]{0:T(1024)(128)(4,1)S(1)}, s32[]{:S(2)}) async-start(s8[6291456]{0:T(1024)(128)(4,1)} %bitcast.12), calls=%async_computation.1 | async-start | bytes 4194304
  21.3 7.1 %collective-permute-start.7 = (s32[1,128]{1,0:T(1,128)S(1)}, s32[1,128]{1,0:T(1,128)S(1)}, u32[]{:S(2)}, u32[]{:S(2)}) collective-permute-start(s32[1,128]{1,0:T(1,128)S(1)} %max.19.known), channel_id=1, source_target_pairs={{0,8},{4,12},{8,0},{12,4},{16,24},{20,28},{24,16},{28,20},{1,9},{5... | collective-permute-start | bytes 1544 | tf_op jit(solution)/shard_map/ppermute | solution.py:365

commit v4 on v3

--- a/solution.py
+++ b/solution.py
@@ -10,7 +10,7 @@
 
 HALF = 128
 ROWS = 512
-LAST_ROWS = 1024
+LAST_ROWS = 256
 WINDOW = 512
 EDGE_WINDOW = 256
 SORT = 256
@@ -258,35 +258,46 @@
 
 
 def last_kernel(
-    own_heads, up_heads, down_heads, near_y, far_y, over, known, field, diag, shear, mean, out, acc,
+    own_heads, up_heads, down_heads, near_y, far_y, over, known, field, diag, shear, mean, out, acc, ready, sems,
     *, bands, tiles_y, scale
 ):
-    block = pl.program_id(0)
-    rows = out.shape[1]
+    rows = LAST_ROWS
     nblocks = bands * HALF // rows
     at_y, odd_z = own_heads[HEAD, 1], own_heads[HEAD, 2] % 2
     odd_y = at_y % 2
     total = jnp.sum(jnp.maximum(known[...], over[...]).astype(jnp.float32), axis=1, keepdims=True)
     amplitude = jnp.sqrt(scale / total) * (1.5 / (HALF * HALF))
-    at_block = pl.ds(pl.multiple_of(block * rows, rows), rows)
-    out[...] = mean[:, at_block, :] + amplitude * field[:, at_block, :]
+
+    def copy_of(block):
+        at = slice(block * rows, (block + 1) * rows)
+        return pltpu.make_async_copy(ready.at[:, at, :], out.at[:, at, :], sems.at[block])
+
+    def fill(block):
+        at = slice(block * rows, (block + 1) * rows)
+        ready[:, at, :] = mean[:, at, :] + amplitude * field[:, at, :]
 
     def add_beyond(heads, tiles, below):
         acc[...] = jnp.zeros_like(acc)
         add_edge(acc, heads, tiles, below, 1 - odd_z, bands)
-        first = pl.multiple_of(below * (bands * HALF - HALF), HALF)
-        parts = transform(diag[:, pl.ds(first, HALF)], shear[:, pl.ds(first, HALF)], acc)
-        at = pl.ds(pl.multiple_of(below * (rows - HALF), HALF), HALF)
-        for c, part in enumerate(parts):
-            out[c, at, :] += amplitude * part
-
-    @pl.when(block == (1 - odd_y) * (nblocks - 1))
-    def _():
-        add_beyond(up_heads, near_y, 1 - odd_y)
-
-    @pl.when((block == odd_y * (nblocks - 1)) & (at_y > 0) & (at_y < tiles_y - 1))
+        at = pl.ds(pl.multiple_of(below * (bands * HALF - HALF), HALF), HALF)
+        for c, part in enumerate(transform(diag[:, at], shear[:, at], acc)):
+            ready[c, at, :] += amplitude * part
+
+    for block in range(1, nblocks - 1):
+        fill(block)
+        copy_of(block).start()
+    fill(0)
+    fill(nblocks - 1)
+    add_beyond(up_heads, near_y, 1 - odd_y)
+
+    @pl.when((at_y > 0) & (at_y < tiles_y - 1))
     def _():
         add_beyond(down_heads, far_y, odd_y)
+
+    copy_of(0).start()
+    copy_of(nblocks - 1).start()
+    for block in range(nblocks):
+        copy_of(block).wait()
 
 
 def with_known(tile, known):
@@ -374,16 +385,18 @@
         compiler_params=params,
     )(own, row_of_tiles, own, row_of_tiles, stress_diag, stress_shear, raw)
 
-    block_rows = LAST_ROWS
-    last_block = pl.BlockSpec((3, block_rows, cols), lambda i: (0, i, 0))
     scale = rows * tiles_y * (cols * tiles_z) / (HALF * HALF)
     return pl.pallas_call(
         functools.partial(last_kernel, bands=bands, tiles_y=tiles_y, scale=scale),
-        grid=(rows // block_rows,),
+        grid=(1,),
         in_specs=[heads] + [edge_heads] * 2 + [vmem] * 8,
-        out_specs=last_block,
+        out_specs=pl.BlockSpec(memory_space=pltpu.HBM),
         out_shape=field_shape,
-        scratch_shapes=[pltpu.VMEM((3, HALF, cols), jnp.float32)],
+        scratch_shapes=[
+            pltpu.VMEM((3, HALF, cols), jnp.float32),
+            pltpu.VMEM((3, rows, cols), jnp.float32),
+            pltpu.SemaphoreType.DMA((rows // LAST_ROWS,)),
+        ],
         cost_estimate=cost(0.3, 2.0),
         compiler_params=pltpu.CompilerParams(vmem_limit_bytes=24 << 20),
     )(

time: 34 us -> 33.1 us (0.974); the launches traced: 33.4 us -> 32.9 us
  Pallas kernels: 17.3 us -> 16.6 us
    pallas_call x1, Pallas kernels: 4.93 us -> 4.26 us  [body(): pl.pallas_call(functools.partial(last_kernel, bands=bands, tiles_y=tiles_...]
where the time goes in v4:
time: 33.1 us; the launch traced here: 32.9 us
  Pallas kernels  16.6 us (50%)
  starting transfers between devices  13.2 us (40%)
  local copies, waits for them, and re-layouts  1.48 us (4%)
  between operations  1 us (3%)
  waiting for transfers between devices  0.45 us (1%)
    pallas_call x1, Pallas kernels, body(): pl.pallas_call(functools.partial(field_kernel, bands=bands), grid=(1,), i...  6.98 us
    ppermute x1, starting transfers between devices, body(): near_y = lax.ppermute(row_of_tiles, 'gy', pairs_near(tiles_y))  4.34 us
    pallas_call x1, Pallas kernels, body(): pl.pallas_call(functools.partial(last_kernel, bands=bands, tiles_y=tiles_...  4.26 us
    ppermute x1, starting transfers between devices, body(): known = jnp.maximum(known, lax.ppermute(known, 'gy', pairs))  4.13 us
    pallas_call x1, Pallas kernels, body(): pl.pallas_call(functools.partial(own_kernel, bands=bands, first=0), grid=...  2.74 us
    pallas_call x1, Pallas kernels, body(): pl.pallas_call(functools.partial(order_kernel, bands=bands, cols=cols), g...  2.61 us
    ppermute x1, starting transfers between devices, body(): one = lax.ppermute(known, 'gy', pairs_near(tiles_y))  1.58 us
    ppermute x1, starting transfers between devices, body(): others.append(lax.ppermute(known, 'gz', pairs_over(tiles_z, by)))  1.56 us
  transfers between devices with their start and end apart: 8, of which 1 were waited for; matrix products, arithmetic and copies ran while one was open for 3% of the time, Pallas kernels for 37%

profile of v4, /device:TPU:0, one launch (start us, length us, event | category | flops | bytes accessed | tf_op | source)
XLA Modules:
  0.0 32.9 jit_solution(10254450412128114008)
XLA Ops:
  0.7 4.1 %collective-permute-start = (s32[1,128]{1,0:T(1,128)S(1)}, s32[1,128]{1,0:T(1,128)S(1)}, u32[]{:S(2)}, u32[]{:S(2)}) collective-permute-start(s32[1,128]{1,0:T(1,128)S(1)} %compare_select_fusion), channel_id=1, source_target_pairs={{0,16},{4,20},{8,24},{12,28},{16,0},{20,4},{24,8},{28,12},{1,17},{... | collective-permute-start | bytes 1544 | tf_op jit(solution)/shard_map/ppermute | solution.py:337
  4.8 0.8 %copy.9 = s32[1,1,3,2048]{3,2,1,0:T(4,128)S(1)} copy(s32[1,1,3,2048]{3,1,2,0:T(1,128)} %param.7) | data formatting | bytes 49152
  5.5 0.0 copy-start.2
  5.6 0.7 %copy-done.2 = s32[1,1,2,2048]{3,2,1,0:T(2,128)S(1)} copy-done((s32[1,1,2,2048]{3,2,1,0:T(2,128)S(1)}, s32[1,1,2,2048]{3,2,1,0:T(2,128)}, u32[]{:S(2)}) %copy-start.2) | copy-done | bytes 16408
  6.3 2.6 %shard_map.64 = s32[8,2048]{1,0:T(8,128)S(1)} custom-call(s32[1,1]{1,0:T(1,128)} %copy.10.count, s32[2,2048]{1,0:T(2,128)S(1)} %bitcast.15, s32[3,2048]{1,0:T(4,128)S(1)} %bitcast.14), custom_call_target="tpu_custom_call" | custom-call | flops 1932735232 | bytes 629145 | tf_op jit(solution)/shard_map/pallas_call | solution.py:338
  8.9 0.0 collective-permute-done
  8.9 1.6 %collective-permute-start.5 = (s32[1,128]{1,0:T(1,128)S(1)}, s32[1,128]{1,0:T(1,128)S(1)}, u32[]{:S(2)}, u32[]{:S(2)}) collective-permute-start(s32[1,128]{1,0:T(1,128)S(1)} %fusion.2), channel_id=1, source_target_pairs={{0,2},{1,3},{2,0},{3,1},{4,6},{5,7},{6,4},{7,5},{8,10},{9,11},{10,... | collective-permute-start | bytes 1544 | tf_op jit(solution)/shard_map/ppermute | solution.py:354
  10.5 0.1 broadcast_select_fusion.own_heads.own
  10.6 0.1 fusion.1
  10.6 0.0 collective-permute-start.2
  10.7 0.6 %collective-permute-start.1 = (s32[8,2048]{1,0:T(8,128)S(1)}, s32[8,2048]{1,0:T(8,128)S(1)}, u32[]{:S(2)}, u32[]{:S(2)}) collective-permute-start(s32[8,2048]{1,0:T(8,128)S(1)} %broadcast_select_fusion.own_heads.own), channel_id=1, source_target_pairs={{0,3},{1,2},{2,1},{3,0},{4,7},{5,6},{6,5},{7,4},{8,11},{9,10},{10,... | collective-permute-start | bytes 196616 | tf_op jit(solution)/shard_map/ppermute | solution.py:350
  11.3 2.7 %shard_map.65.raw = f32[3,1024,256]{2,1,0:T(8,128)S(1)} custom-call(s32[8,2048]{1,0:T(8,128)S(1)} %broadcast_select_fusion.own_heads.own, s32[8,2048]{1,0:T(8,128)S(1)} %broadcast_select_fusion.own_heads.own), custom_call_target="tpu_custom_call" | custom-call | flops 1288490240 | bytes 3145728 | tf_op jit(solution)/shard_map/pallas_call | solution.py:365
  14.1 0.0 collective-permute-done.5
  14.1 0.0 collective-permute-done.2
  14.1 0.4 %collective-permute-done.1 = s32[8,2048]{1,0:T(8,128)S(1)} collective-permute-done((s32[8,2048]{1,0:T(8,128)S(1)}, s32[8,2048]{1,0:T(8,128)S(1)}, u32[]{:S(2)}, u32[]{:S(2)}) %collective-permute-start.1) | collective-permute-done | bytes 65568 | tf_op jit(solution)/shard_map/ppermute | solution.py:350
  14.5 1.6 %collective-permute-start.6 = (s32[1,128]{1,0:T(1,128)S(1)}, s32[1,128]{1,0:T(1,128)S(1)}, u32[]{:S(2)}, u32[]{:S(2)}) collective-permute-start(s32[1,128]{1,0:T(1,128)S(1)} %fusion), channel_id=1, source_target_pairs={{0,4},{4,0},{8,12},{12,8},{16,20},{20,16},{24,28},{28,24},{1,5},{5... | collective-permute-start | bytes 1544 | tf_op jit(solution)/shard_map/ppermute | solution.py:357
  16.1 0.9 %collective-permute-start.4 = (s32[3,8,2048]{2,1,0:T(8,128)S(1)}, s32[3,8,2048]{2,1,0:T(8,128)S(1)}, u32[]{:S(2)}, u32[]{:S(2)}) collective-permute-start(s32[3,8,2048]{2,1,0:T(8,128)S(1)} %pad_add_fusion.heads.tiles), channel_id=1, source_target_pairs={{4,8},{8,4},{12,16},{16,12},{20,24},{24,20},{5,9},{9,5},{13,17},{1... | collective-permute-start | bytes 589832 | tf_op jit(solution)/shard_map/ppermute | solution.py:359
  17.0 4.3 %collective-permute-start.3 = (s32[3,8,2048]{2,1,0:T(8,128)S(1)}, s32[3,8,2048]{2,1,0:T(8,128)S(1)}, u32[]{:S(2)}, u32[]{:S(2)}) collective-permute-start(s32[3,8,2048]{2,1,0:T(8,128)S(1)} %pad_add_fusion.heads.tiles), channel_id=1, source_target_pairs={{0,4},{4,0},{8,12},{12,8},{16,20},{20,16},{24,28},{28,24},{1,5},{5... | collective-permute-start | bytes 589832 | tf_op jit(solution)/shard_map/ppermute | solution.py:358
  21.3 0.0 collective-permute-done.6
  21.3 0.1 collective-permute-start.7
  21.4 7.0 %shard_map.66.field = f32[3,2048,256]{2,1,0:T(8,128)S(1)} custom-call(s32[8,2048]{1,0:T(8,128)S(1)} %broadcast_select_fusion.own_heads.own, s32[3,8,2048]{2,1,0:T(8,128)S(1)} %pad_add_fusion.heads.tiles, s32[8,2048]{1,0:T(8,128)S(1)} %broadcast_select_fusion.own_heads.own, s32[3,8,2048]{2,1,0:T(8,128)S(1)} %pad_add_fusion.heads.tiles, ...), custom_call_target="tpu_custom_call" | custom-call | flops 2576980480 | bytes 6291456 | tf_op jit(solution)/shard_map/pallas_call | solution.py:377
  28.4 0.0 collective-permute-done.4.down_heads.far_y
  28.4 0.0 collective-permute-done.3.up_heads.near_y
  28.5 4.3 %shard_map.67 = f32[3,2048,256]{2,1,0:T(8,128)} custom-call(s32[8,2048]{1,0:T(8,128)S(1)} %broadcast_select_fusion.own_heads.own, s32[3,8,2048]{2,1,0:T(8,128)S(1)} %collective-permute-done.3.up_heads.near_y, s32[3,8,2048]{2,1,0:T(8,128)S(1)} %collective-permute-done.4.down_heads.far_y, s32[3,8,2048]{2,1,0:T(8,128)S(1)} %collective-permute-done.3.up_heads.near_y, ...), custom_call_target="tpu_custom_call" | custom-call | flops 1932735232 | bytes 12582912 | tf_op jit(solution)/shard_map/pallas_call | solution.py:389
  (17 shorter events, 0.1 us)
Async XLA Ops:
  0.7 8.2 %collective-permute-start = (s32[1,128]{1,0:T(1,128)S(1)}, s32[1,128]{1,0:T(1,128)S(1)}, u32[]{:S(2)}, u32[]{:S(2)}) collective-permute-start(s32[1,128]{1,0:T(1,128)S(1)} %compare_select_fusion), channel_id=1, source_target_pairs={{0,16},{4,20},{8,24},{12,28},{16,0},{20,4},{24,8},{28,12},{1,17},{... | collective-permute-start | bytes 1544 | tf_op jit(solution)/shard_map/ppermute | solution.py:337
  5.5 0.7 %copy-start.2 = (s32[1,1,2,2048]{3,2,1,0:T(2,128)S(1)}, s32[1,1,2,2048]{3,2,1,0:T(2,128)}, u32[]{:S(2)}) copy-start(s32[1,1,2,2048]{3,2,1,0:T(2,128)} %param.6) | copy-start | bytes 49156
  6.3 15.1 %copy-start = (f32[3,2048]{1,0:T(4,128)S(1)}, f32[3,2048]{1,0:T(4,128)}, u32[]{:S(2)}) copy-start(f32[3,2048]{1,0:T(4,128)} %diag.3) | copy-start | bytes 73732
  6.3 15.1 %copy-start.1 = (f32[3,2048]{1,0:T(4,128)S(1)}, f32[3,2048]{1,0:T(4,128)}, u32[]{:S(2)}) copy-start(f32[3,2048]{1,0:T(4,128)} %shear.3) | copy-start | bytes 73732
  8.9 5.1 %collective-permute-start.5 = (s32[1,128]{1,0:T(1,128)S(1)}, s32[1,128]{1,0:T(1,128)S(1)}, u32[]{:S(2)}, u32[]{:S(2)}) collective-permute-start(s32[1,128]{1,0:T(1,128)S(1)} %fusion.2), channel_id=1, source_target_pairs={{0,2},{1,3},{2,0},{3,1},{4,6},{5,7},{6,4},{7,5},{8,10},{9,11},{10,... | collective-permute-start | bytes 1544 | tf_op jit(solution)/shard_map/ppermute | solution.py:354
  10.6 3.4 %collective-permute-start.2 = (s32[8,2048]{1,0:T(8,128)S(1)}, s32[8,2048]{1,0:T(8,128)S(1)}, u32[]{:S(2)}, u32[]{:S(2)}) collective-permute-start(s32[8,2048]{1,0:T(8,128)S(1)} %broadcast_select_fusion.own_heads.own), channel_id=1, source_target_pairs={{0,1},{1,0},{2,3},{3,2},{4,5},{5,4},{6,7},{7,6},{8,9},{9,8},{10,11... | collective-permute-start | bytes 196616 | tf_op jit(solution)/shard_map/ppermute | solution.py:349
  10.7 3.8 %collective-permute-start.1 = (s32[8,2048]{1,0:T(8,128)S(1)}, s32[8,2048]{1,0:T(8,128)S(1)}, u32[]{:S(2)}, u32[]{:S(2)}) collective-permute-start(s32[8,2048]{1,0:T(8,128)S(1)} %broadcast_select_fusion.own_heads.own), channel_id=1, source_target_pairs={{0,3},{1,2},{2,1},{3,0},{4,7},{5,6},{6,5},{7,4},{8,11},{9,10},{10,... | collective-permute-start | bytes 196616 | tf_op jit(solution)/shard_map/ppermute | solution.py:350
  11.3 17.1 %slice-start = ((s8[6291456]{0:T(1024)(128)(4,1)}), s8[4194304]{0:T(1024)(128)(4,1)S(1)}, s32[]{:S(2)}) async-start(s8[6291456]{0:T(1024)(128)(4,1)} %bitcast.12), calls=%async_computation | async-start | bytes 8388608
  14.5 6.8 %collective-permute-start.6 = (s32[1,128]{1,0:T(1,128)S(1)}, s32[1,128]{1,0:T(1,128)S(1)}, u32[]{:S(2)}, u32[]{:S(2)}) collective-permute-start(s32[1,128]{1,0:T(1,128)S(1)} %fusion), channel_id=1, source_target_pairs={{0,4},{4,0},{8,12},{12,8},{16,20},{20,16},{24,28},{28,24},{1,5},{5... | collective-permute-start | bytes 1544 | tf_op jit(solution)/shard_map/ppermute | solution.py:357
  16.1 12.3 %collective-permute-start.4 = (s32[3,8,2048]{2,1,0:T(8,128)S(1)}, s32[3,8,2048]{2,1,0:T(8,128)S(1)}, u32[]{:S(2)}, u32[]{:S(2)}) collective-permute-start(s32[3,8,2048]{2,1,0:T(8,128)S(1)} %pad_add_fusion.heads.tiles), channel_id=1, source_target_pairs={{4,8},{8,4},{12,16},{16,12},{20,24},{24,20},{5,9},{9,5},{13,17},{1... | collective-permute-start | bytes 589832 | tf_op jit(solution)/shard_map/ppermute | solution.py:359
  17.0 11.5 %collective-permute-start.3 = (s32[3,8,2048]{2,1,0:T(8,128)S(1)}, s32[3,8,2048]{2,1,0:T(8,128)S(1)}, u32[]{:S(2)}, u32[]{:S(2)}) collective-permute-start(s32[3,8,2048]{2,1,0:T(8,128)S(1)} %pad_add_fusion.heads.tiles), channel_id=1, source_target_pairs={{0,4},{4,0},{8,12},{12,8},{16,20},{20,16},{24,28},{28,24},{1,5},{5... | collective-permute-start | bytes 589832 | tf_op jit(solution)/shard_map/ppermute | solution.py:358
  21.3 7.1 %slice-start.1 = ((s8[6291456]{0:T(1024)(128)(4,1)}), s8[2097152]{0:T(1024)(128)(4,1)S(1)}, s32[]{:S(2)}) async-start(s8[6291456]{0:T(1024)(128)(4,1)} %bitcast.12), calls=%async_computation.1 | async-start | bytes 4194304
  21.3 7.1 %collective-permute-start.7 = (s32[1,128]{1,0:T(1,128)S(1)}, s32[1,128]{1,0:T(1,128)S(1)}, u32[]{:S(2)}, u32[]{:S(2)}) collective-permute-start(s32[1,128]{1,0:T(1,128)S(1)} %max.19.known), channel_id=1, source_target_pairs={{0,8},{4,12},{8,0},{12,4},{16,24},{20,28},{24,16},{28,20},{1,9},{5... | collective-permute-start | bytes 1544 | tf_op jit(solution)/shard_map/ppermute | solution.py:376
